TPU v7x, 32 devices: a whole 2x2x4 slice. The times are simulated.
32 devices in a mesh: kgrp: 2 (over y), band: 4 (over z), fft: 4 (over x, core).
Axes of the slice: x: 2, y: 2, z: 4, core: 2. Of those that a mesh axis runs over, the one named last changes fastest.
Arguments:
- orbitals: float32 [8, 64, 64, 128], P(('kgrp', 'band'), 'fft'), parts along dimension 0, may hold values from -6 to 6
- partners: float32 [8, 64, 64, 128], P(('kgrp', 'band'), 'fft'), parts along dimension 0, may hold values from -6 to 6
- shift_table: float32 [8, 3], replicated, may hold values from -0.5 to 0.5
- shift_index: int32 [8], P('kgrp'), parts along dimension 0, may hold values from 0 to 7
Outputs:
- potential: float32 [8, 64, 64, 128], P(('kgrp', 'band'), 'fft'), parts along dimension 0
- projector: float32 [8, 64, 64, 128], P(('kgrp', 'band'), 'fft'), parts along dimension 0
There are 2 independent parts, one for each index of `kgrp`. A program takes and returns all parts, laid end to end along the dimension named above; an argument that names none is the same for every part. Nothing has to cross between parts.
All inputs are finite; a program needn't handle non-finite values.
Results may differ from a plain program's by a relative error of at most 0.0001.
Values sent between devices are 32-bit elements; how exact they have to be, the bound alone decides.
A program may use at most 64 MiB of HBM per device.

v0:
```python
import functools
import math

import jax
import jax.numpy as jnp
import numpy as np
from jax import lax
from jax.experimental import pallas as pl
from jax.experimental.pallas import tpu as pltpu
from jax.sharding import PartitionSpec as P

HIGHEST = lax.Precision.HIGHEST
HIGH = lax.Precision.HIGH
MESH = pl.DeviceIdType.MESH
GROUP = 8
SCREEN_SQUARE = 0.25
FOUR_PI = 4.0 * math.pi


def angle_pair(extent, sign):
    positions = jnp.arange(extent, dtype=jnp.int32)
    product = positions[:, None] * positions[None, :] % extent
    angle = 2.0 * math.pi / extent * product.astype(jnp.float32)
    return (jnp.cos(angle), sign * jnp.sin(angle))


def last_table(extent, sign):
    cosine, sine = angle_pair(extent, sign)
    upper = jnp.concatenate([cosine, sine], axis=1)
    lower = jnp.concatenate([-sine, cosine], axis=1)
    return jnp.concatenate([upper, lower], axis=0)


def middle_table(extent, sign):
    cosine, sine = angle_pair(extent, sign)
    return jnp.stack([jnp.stack([cosine, -sine], -1), jnp.stack([sine, cosine], -1)], 1)


def along_last(field, table):
    shape = field.shape
    flat = field.reshape(-1, shape[-1])
    return jnp.dot(flat, table, precision=HIGH).reshape(shape)


def along_axis(field, table, axis_number):
    shape = field.shape
    extent = shape[-1] // 2
    split = field.reshape(shape[0], shape[1], shape[2], 2, extent)
    if axis_number == 1:
        result = jnp.einsum("kcnd,pnbdz->pkbcz", table, split, precision=HIGH)
    else:
        result = jnp.einsum("kcnd,pandz->pakcz", table, split, precision=HIGH)
    return result.reshape(shape)


def times_conj(left, right):
    extent = left.shape[-1] // 2
    left_real, left_imag = (left[..., :extent], left[..., extent:])
    right_real, right_imag = (right[..., :extent], right[..., extent:])
    return jnp.concatenate(
        [
            left_real * right_real + left_imag * right_imag,
            left_real * right_imag - left_imag * right_real,
        ],
        axis=-1,
    )


def times(left, right):
    extent = left.shape[-1] // 2
    left_real, left_imag = (left[..., :extent], left[..., extent:])
    right_real, right_imag = (right[..., :extent], right[..., extent:])
    return jnp.concatenate(
        [
            left_real * right_real - left_imag * right_imag,
            left_real * right_imag + left_imag * right_real,
        ],
        axis=-1,
    )


def rotate(field):
    extent = field.shape[-1] // 2
    return jnp.concatenate([field[..., extent:], -field[..., :extent]], axis=-1)


def frequency(positions, extent):
    return jnp.where(positions < extent // 2, positions, positions - extent).astype(jnp.float32)


def kernel_block(qvectors, y_count, extent):
    first_freq = frequency(jnp.arange(extent, dtype=jnp.int32), extent)
    second_freq = frequency(jnp.arange(y_count, dtype=jnp.int32), extent)
    third_freq = frequency(jnp.arange(2 * extent, dtype=jnp.int32) % extent, extent)
    first_part = (first_freq[None, :] + qvectors[:, 0:1]) ** 2
    second_part = (second_freq[None, :] + qvectors[:, 1:2]) ** 2
    third_part = (third_freq[None, :] + qvectors[:, 2:3]) ** 2
    denominator = (
        first_part[:, :, None, None]
        + second_part[:, None, :, None]
        + third_part[:, None, None, :]
        + SCREEN_SQUARE
    )
    return FOUR_PI / extent**3 / denominator


def shifts_for(shift_table, shift_index, start_at, length):
    picked = lax.dynamic_slice_in_dim(shift_index, start_at, length)
    onehot = (picked[:, None] == jnp.arange(shift_table.shape[0], dtype=jnp.int32)[None, :]).astype(
        jnp.float32
    )
    return jnp.dot(onehot, shift_table, precision=HIGHEST)


def factor_inverse(over_real, over_imag):
    matrix_order = over_real.shape[0]
    positions = jnp.arange(matrix_order, dtype=jnp.int32)
    zero_start = jnp.zeros_like(over_real)

    def chol_step(column, lowers):
        lower_real, lower_imag = lowers
        row_real = lower_real[column]
        row_imag = lower_imag[column]
        resid_real = over_real[:, column] - (
            jnp.dot(lower_real, row_real, precision=HIGHEST)
            + jnp.dot(lower_imag, row_imag, precision=HIGHEST)
        )
        resid_imag = over_imag[:, column] - (
            jnp.dot(lower_imag, row_real, precision=HIGHEST)
            - jnp.dot(lower_real, row_imag, precision=HIGHEST)
        )
        pivot_value = jnp.sqrt(resid_real[column])
        below_diag = positions > column
        at_diag = positions == column
        new_real = jnp.where(
            below_diag, resid_real / pivot_value, jnp.where(at_diag, pivot_value, 0.0)
        )
        new_imag = jnp.where(below_diag, resid_imag / pivot_value, 0.0)
        chosen = positions[None, :] == column
        return (
            jnp.where(chosen, new_real[:, None], lower_real),
            jnp.where(chosen, new_imag[:, None], lower_imag),
        )

    lower_real, lower_imag = lax.fori_loop(0, matrix_order, chol_step, (zero_start, zero_start))

    def solve_step(row_index, inverses):
        inv_real, inv_imag = inverses
        row_real = lower_real[row_index]
        row_imag = lower_imag[row_index]
        sum_real = jnp.dot(row_real, inv_real, precision=HIGHEST) - jnp.dot(
            row_imag, inv_imag, precision=HIGHEST
        )
        sum_imag = jnp.dot(row_real, inv_imag, precision=HIGHEST) + jnp.dot(
            row_imag, inv_real, precision=HIGHEST
        )
        unit_row = (positions == row_index).astype(over_real.dtype)
        pivot_value = lower_real[row_index, row_index]
        new_real = (unit_row - sum_real) / pivot_value
        new_imag = -sum_imag / pivot_value
        chosen = positions[:, None] == row_index
        return (
            jnp.where(chosen, new_real[None, :], inv_real),
            jnp.where(chosen, new_imag[None, :], inv_imag),
        )

    return lax.fori_loop(0, matrix_order, solve_step, (zero_start, zero_start))


def general_body(orbitals, partners, shift_table, shift_index):
    extent = orbitals.shape[2]
    band_count = orbitals.shape[0]
    tables = (
        last_table(extent, -1.0),
        middle_table(extent, -1.0),
        last_table(extent, 1.0),
        middle_table(extent, 1.0),
    )
    my_band = lax.axis_index("band")
    forward_last, forward_mid, inverse_last, inverse_mid = tables
    full_orbitals = lax.all_gather(orbitals, "fft", axis=1, tiled=True)
    every_slab = lax.all_gather(partners, "band", axis=0, tiled=True)
    own_grids = lax.all_to_all(every_slab, "fft", split_axis=0, concat_axis=1, tiled=True)
    own_count = own_grids.shape[0]
    qvectors = shifts_for(shift_table, shift_index, lax.axis_index("fft") * own_count, own_count)

    def one_partner(member, running):
        single = lax.dynamic_slice_in_dim(own_grids, member, 1, 0)
        kernel = kernel_block(lax.dynamic_slice_in_dim(qvectors, member, 1, 0), extent, extent)
        density = times_conj(single, full_orbitals)
        spectrum = (
            along_axis(
                along_axis(along_last(density, forward_last), forward_mid, 2), forward_mid, 1
            )
            * kernel
        )
        field = along_last(
            along_axis(along_axis(spectrum, inverse_mid, 1), inverse_mid, 2), inverse_last
        )
        return running + times(single, field)

    partial_value = lax.fori_loop(
        0, own_count, one_partner, jnp.zeros(full_orbitals.shape, jnp.float32)
    )
    potential = lax.psum_scatter(partial_value, "fft", scatter_dimension=1, tiled=True)
    every_pot = lax.all_gather(potential, "band", axis=0, tiled=True)
    turned = rotate(every_pot)
    total_bands = every_pot.shape[0]
    flat_orbitals = orbitals.reshape(band_count, -1)
    flat_pot = every_pot.reshape(total_bands, -1)
    flat_turned = turned.reshape(total_bands, -1)
    volume = float(extent**3)
    rows_real = jnp.einsum("ik,jk->ij", flat_orbitals, flat_pot, precision=HIGHEST) / volume
    rows_imag = jnp.einsum("ik,jk->ij", flat_orbitals, flat_turned, precision=HIGHEST) / volume
    start_row = my_band * band_count
    summed_real, summed_imag = lax.psum((rows_real, rows_imag), "fft")
    over_real, over_imag = (
        lax.all_gather(summed_real, "band", axis=0, tiled=True),
        lax.all_gather(summed_imag, "band", axis=0, tiled=True),
    )
    inv_real, inv_imag = factor_inverse(over_real, over_imag)
    coef_real = lax.dynamic_slice_in_dim(inv_real, start_row, band_count, 0)
    coef_imag = lax.dynamic_slice_in_dim(inv_imag, start_row, band_count, 0)
    projector = jnp.dot(coef_real, flat_pot, precision=HIGHEST) + jnp.dot(
        coef_imag, flat_turned, precision=HIGHEST
    )
    return (potential, projector.reshape(orbitals.shape))


def remote(source, target, send_sem, recv_sem, where):
    return pltpu.make_async_remote_copy(
        src_ref=source,
        dst_ref=target,
        send_sem=send_sem,
        recv_sem=recv_sem,
        device_id=where,
        device_id_type=MESH,
    )


def greet(others):
    barrier = pltpu.get_barrier_semaphore()
    for other in others:
        pl.semaphore_signal(barrier, inc=1, device_id=other, device_id_type=MESH)
    pl.semaphore_wait(barrier, len(others))


def turn(block):
    lanes = block.shape[-1]
    swapped = pltpu.roll(block, lanes // 2, block.ndim - 1)
    position = lax.broadcasted_iota(jnp.int32, block.shape, block.ndim - 1)
    return jnp.where(position < lanes // 2, swapped, -swapped)


def small_factor_inverse(matrix):
    order = len(matrix)
    lower = [[None] * order for _ in range(order)]
    for column in range(order):
        residual = []
        for row in range(column, order):
            real, imag = matrix[row][column]
            for k in range(column):
                a, b = lower[row][k]
                c, d = lower[column][k]
                real = real - (a * c + b * d)
                imag = imag - (b * c - a * d)
            residual.append((real, imag))
        pivot = jnp.sqrt(residual[0][0])
        lower[column][column] = (pivot, jnp.zeros_like(pivot))
        for row in range(column + 1, order):
            real, imag = residual[row - column]
            lower[row][column] = (real / pivot, imag / pivot)
    inverse = [[None] * order for _ in range(order)]
    for row in range(order):
        pivot = lower[row][row][0]
        inverse[row][row] = (1.0 / pivot, jnp.zeros_like(pivot))
        for column in range(row):
            real = jnp.zeros_like(pivot)
            imag = jnp.zeros_like(pivot)
            for k in range(column, row):
                a, b = lower[row][k]
                c, d = inverse[k][column]
                real = real - (a * c - b * d)
                imag = imag - (a * d + b * c)
            inverse[row][column] = (real / pivot, imag / pivot)
    return inverse


def split_table(table):
    high = table.astype(jnp.bfloat16)
    low = (table - high.astype(np.float64)).astype(jnp.bfloat16)
    return high, low


def right_table(extent, sign):
    grid = np.outer(np.arange(extent), np.arange(extent)) % extent
    angle = 2.0 * math.pi / extent * grid
    cosine, sine = np.cos(angle), sign * np.sin(angle)
    table = np.block([[cosine, sine], [-sine, cosine]])
    high, low = split_table(table)
    upper = np.concatenate([high, low], axis=1)
    lower = np.concatenate([high, np.zeros_like(low)], axis=1)
    return np.concatenate([upper, lower], axis=0)


def left_table(extent, sign):
    grid = np.outer(np.arange(extent), np.arange(extent)) % extent
    angle = 2.0 * math.pi / extent * grid
    high, low = split_table(np.concatenate([np.cos(angle), sign * np.sin(angle)], axis=0))
    return np.concatenate([high, high, low], axis=1)


def halves(value):
    high = value.astype(jnp.bfloat16)
    low = (value - high.astype(jnp.float32)).astype(jnp.bfloat16)
    return high, low


def right_product(value, table):
    lanes = value.shape[-1]
    high, low = halves(value)
    both = jnp.dot(
        jnp.concatenate([high, low], axis=1), table, preferred_element_type=jnp.float32
    )
    return both[:, :lanes] + both[:, lanes:]


def left_product(first, second, table):
    rows, lanes = first.shape
    high, low = halves(jnp.concatenate([first, second], axis=1))
    stacked = jnp.concatenate([high, low, high], axis=0)
    both = jnp.dot(table, stacked, preferred_element_type=jnp.float32)
    return tuple(
        both[:rows, cut : cut + lanes] - turn(both[rows:, cut : cut + lanes])
        for cut in (0, lanes)
    )


def spread_parts(value):
    lanes = value.shape[-1]
    swapped = pltpu.roll(value, lanes // 2, value.ndim - 1)
    lower = lax.broadcasted_iota(jnp.int32, value.shape, value.ndim - 1) < lanes // 2
    return jnp.where(lower, value, swapped), jnp.where(lower, swapped, value)


def forward_group(group, orbital_grid, partner_grid, work, right, left):
    rows, lanes = orbital_grid.shape[1:]
    span = pl.ds(group * GROUP, GROUP)
    orbital = orbital_grid[span].reshape(GROUP * rows, lanes)
    real, imag = spread_parts(partner_grid[span].reshape(GROUP * rows, lanes))
    density = real * orbital + imag * turn(orbital)
    lines = right_product(density, right[...])
    planes = []
    for pair in range(GROUP // 2):
        start = 2 * pair * rows
        planes += left_product(
            lines[start : start + rows], lines[start + rows : start + 2 * rows], left[...]
        )
    stacked = jnp.stack(planes, axis=0)
    work[:, span, :] = jnp.swapaxes(stacked, 0, 1)


def backward_group(group, partner_grid, partial, work, right, left):
    rows, lanes = partner_grid.shape[1:]
    span = pl.ds(group * GROUP, GROUP)
    planes = jnp.swapaxes(work[:, span, :], 0, 1)
    lines = []
    for pair in range(GROUP // 2):
        lines += left_product(planes[2 * pair], planes[2 * pair + 1], left[...])
    field = right_product(jnp.concatenate(lines, axis=0), right[...])
    real, imag = spread_parts(partner_grid[span].reshape(GROUP * rows, lanes))
    partial[span] = (real * field - imag * turn(field)).reshape(GROUP, rows, lanes)


def middle_pairs(shift, work, forward, inverse):
    columns, extent, lanes = work.shape
    first = frequency(lax.broadcasted_iota(jnp.int32, (extent, lanes), 0), extent)
    third_place = lax.broadcasted_iota(jnp.int32, (extent, lanes), 1)
    third_place = jnp.where(third_place < lanes // 2, third_place, third_place - lanes // 2)
    third = frequency(third_place, extent)
    base = (first + shift[0]) ** 2 + (third + shift[2]) ** 2 + SCREEN_SQUARE
    scale = FOUR_PI / (float(extent) * float(columns) * float(lanes // 2))

    def one_pair(pair, carry):
        spectra = left_product(work[2 * pair], work[2 * pair + 1], forward[...])
        scaled = []
        for which in range(2):
            column = 2 * pair + which
            second = jnp.where(column < columns // 2, column, column - columns)
            offset = (second.astype(jnp.float32) + shift[1]) ** 2
            scaled.append(spectra[which] * (scale / (base + offset)))
        fields = left_product(scaled[0], scaled[1], inverse[...])
        work[2 * pair] = fields[0]
        work[2 * pair + 1] = fields[1]
        return carry

    lax.fori_loop(0, columns // 2, one_pair, 0, unroll=4)


def exchange_kernel(
    bands,
    ranks,
    shift_table,
    shift_index,
    orbital_home,
    partner_home,
    right_forward_home,
    right_inverse_home,
    left_forward_home,
    left_inverse_home,
    potential,
    projector,
    orbital_grid,
    partner_grid,
    orbital_parts,
    from_below,
    from_above,
    work,
    partial,
    near,
    outgoing,
    arriving,
    potential_parts,
    projector_parts,
    own_sums,
    all_sums,
    chain_send,
    chain_recv,
    deliver_send,
    deliver_recv,
    grid_send,
    grid_recv,
    early_send,
    early_recv,
    local_sem,
    near_send,
    near_recv,
    far_send,
    far_recv,
    part_send,
    part_recv,
    sum_send,
    sum_recv,
    back_send,
    back_recv,
    orbital,
    partner,
    right_forward,
    right_inverse,
    left_forward,
    left_inverse,
    load_sem,
):
    loads = [
        pltpu.make_async_copy(home, here, load_sem.at[number])
        for number, (home, here) in enumerate(
            (
                (partner_home, partner),
                (orbital_home, orbital),
                (right_forward_home, right_forward),
                (left_forward_home, left_forward),
                (right_inverse_home, right_inverse),
                (left_inverse_home, left_inverse),
            )
        )
    ]
    for load in loads:
        load.start()
    band = lax.axis_index("band")
    rank = lax.axis_index("fft")
    planes, rows, lanes = orbital.shape
    piece = planes // bands
    per_group = GROUP // piece
    halves_count = planes // GROUP
    greet(
        [
            {"band": (band + step) % bands, "fft": (rank + turn_by) % ranks}
            for step in range(bands)
            for turn_by in range(ranks)
            if step or turn_by
        ]
    )
    loads[0].wait()

    def span(index):
        return pl.ds(index * piece, piece)

    def slab(index):
        return pl.ds(index * planes, planes)

    beside = rank + 1 - 2 * (rank % 2)
    across = (rank + 2) % ranks
    beside_across = (beside + 2) % ranks

    def chain_copy(upward, distance, chunk):
        held = from_below if upward else from_above
        source = partner.at[span(chunk)] if distance == 0 else held.at[distance - 1, chunk]
        way = 0 if upward else 1
        return remote(
            source,
            held.at[distance, chunk],
            chain_send.at[way, distance, chunk],
            chain_recv.at[way, distance, chunk],
            {"band": band + 1 if upward else band - 1},
        )

    def deliver(upward, distance, chunk, act):
        held = from_below if upward else from_above
        source = partner.at[span(chunk)] if distance == 0 else held.at[distance - 1, chunk]
        owner = band - distance if upward else band + distance
        target = partner_grid.at[pl.ds(rank * planes + chunk * piece, piece)]
        way = 0 if upward else 1

        @pl.when(owner == rank)
        def _():
            if act == "start":
                pltpu.make_async_copy(source, target, local_sem.at[chunk]).start()

        @pl.when(owner != rank)
        def _():
            copy = remote(
                source,
                target,
                deliver_send.at[way, distance, chunk],
                deliver_recv.at[rank, chunk],
                {"fft": owner},
            )
            copy.start() if act == "start" else copy.wait_send()

    def has_source(upward, distance):
        return band >= distance if upward else band + distance <= bands - 1

    def has_next(upward):
        return band <= bands - 2 if upward else band >= 1

    def both(first, second):
        return jnp.logical_and(first, second)

    def forward_half(half):
        for chunk in range(half * per_group, (half + 1) * per_group):
            target = partner_grid.at[pl.ds(rank * planes + chunk * piece, piece)]
            pltpu.make_async_copy(partner.at[span(chunk)], target, local_sem.at[chunk]).wait()
            for step in range(1, ranks):
                source = (rank + step) % ranks
                target = partner_grid.at[pl.ds(source * planes + chunk * piece, piece)]
                remote(
                    target,
                    target,
                    deliver_send.at[0, 0, chunk],
                    deliver_recv.at[source, chunk],
                    {"fft": source},
                ).wait_recv()

        def forward(index, carry):
            forward_group(
                index * halves_count + half,
                orbital_grid,
                partner_grid,
                work,
                right_forward,
                left_forward,
            )
            return carry

        lax.fori_loop(0, ranks, forward, 0)

    for chunk in range(bands):
        for upward in (True, False):

            @pl.when(has_next(upward))
            def _():
                chain_copy(upward, 0, chunk).start()

    loads[1].wait()
    to_across = remote(
        orbital, orbital_grid.at[slab(rank)], grid_send.at[0], grid_recv.at[0], {"fft": across}
    )
    to_beside = remote(
        orbital, orbital_grid.at[slab(rank)], grid_send.at[1], grid_recv.at[1], {"fft": beside}
    )
    to_across.start()
    to_beside.start()
    own_grid = pltpu.make_async_copy(orbital, orbital_grid.at[slab(rank)], local_sem.at[bands])
    own_grid.start()
    for chunk in range(bands):
        deliver(True, 0, chunk, "start")
    onward = remote(
        orbital_grid.at[slab(across)],
        orbital_grid.at[slab(across)],
        grid_send.at[2],
        grid_recv.at[2],
        {"fft": beside},
    )
    for distance in range(1, bands):
        for chunk in range(bands):
            for upward in (True, False):

                @pl.when(has_source(upward, distance))
                def _():
                    chain_copy(upward, distance - 1, chunk).wait_recv()

                if distance < bands - 1:

                    @pl.when(both(has_source(upward, distance), has_next(upward)))
                    def _():
                        chain_copy(upward, distance, chunk).start()

                @pl.when(has_source(upward, distance))
                def _():
                    deliver(upward, distance, chunk, "start")

            if distance == bands - 1 and chunk > 0 and chunk % per_group == 0:
                forward_half(chunk // per_group - 1)

        if distance == 1:
            to_across.wait_recv()
            onward.start()
            own_grid.wait()
            for load in loads[2:]:
                load.wait()
            to_beside.wait_recv()
            onward.wait_recv()
    forward_half(halves_count - 1)
    early_copies = []
    for step in range(1, bands):
        other = (band + step) % bands
        copy = remote(
            orbital.at[span(other)],
            orbital_parts.at[band],
            early_send.at[step - 1],
            early_recv.at[step - 1],
            {"band": other},
        )
        copy.start()
        early_copies.append(copy)
    own_part = pltpu.make_async_copy(
        orbital.at[span(band)], orbital_parts.at[band], local_sem.at[bands + 1]
    )
    own_part.start()

    chosen = shift_index[rank]
    shift = [shift_table[chosen, axis] for axis in range(3)]
    middle_pairs(shift, work, left_forward, left_inverse)

    def backward_slab(index):
        def backward(half, carry):
            backward_group(
                index * halves_count + half, partner_grid, partial, work, right_inverse, left_inverse
            )
            return carry

        lax.fori_loop(0, halves_count, backward, 0)

    def near_copy(which, index):
        return remote(
            partial.at[slab(index)],
            near.at[which],
            near_send.at[which],
            near_recv.at[which],
            {"fft": beside},
        )

    def far_copy(chunk):
        return remote(
            outgoing.at[chunk],
            arriving.at[chunk],
            far_send.at[chunk],
            far_recv.at[chunk],
            {"fft": across},
        )

    def window(index, chunk):
        return pl.ds(index * planes + chunk * piece, piece)

    turns = [(band + step) % bands for step in range(1, bands + 1)]
    backward_slab(beside_across)
    near_copy(1, beside_across).start()
    backward_slab(across)
    near_copy(1, beside_across).wait_recv()
    for chunk in turns:
        outgoing[chunk] = partial[window(across, chunk)] + near[1, span(chunk)]
        far_copy(chunk).start()
    backward_slab(beside)
    near_copy(0, beside).start()
    backward_slab(rank)
    near_copy(0, beside).wait_recv()

    def part_copy(chunk):
        return remote(
            potential.at[span(chunk)],
            potential_parts.at[band],
            part_send.at[chunk],
            part_recv.at[band],
            {"band": chunk},
        )

    for step, chunk in enumerate(turns):
        far_copy(chunk).wait_recv()
        potential[span(chunk)] = (
            partial[window(rank, chunk)] + near[0, span(chunk)]
        ) + arriving[chunk]
        if step < bands - 1:
            part_copy(chunk).start()
        else:
            potential_parts[band] = potential[span(band)]
    for chunk in turns[:-1]:
        remote(
            potential_parts.at[chunk],
            potential_parts.at[chunk],
            part_send.at[chunk],
            part_recv.at[chunk],
            {"band": chunk},
        ).wait_recv()
    for copy in early_copies:
        copy.wait()
    own_part.wait()

    entries = [(i, l) for i in range(bands) for l in range(i + 1)]
    position = lax.broadcasted_iota(jnp.int32, (8, lanes), 1)

    def accumulate(plane, sums):
        turned = []
        straight = []
        for l in range(bands):
            block = potential_parts[l, plane]
            straight.append(block)
            turned.append(turn(block))
        result = []
        for number, (i, l) in enumerate(entries):
            left = orbital_parts[i, plane]
            for half, right in enumerate((straight[l], turned[l])):
                product = (left * right).reshape(rows // 8, 8, lanes)
                result.append(sums[2 * number + half] + jnp.sum(product, axis=0))
        return tuple(result)

    zero = jnp.zeros((8, lanes), jnp.float32)
    sums = lax.fori_loop(0, piece, accumulate, (zero,) * (2 * len(entries)))
    packed = zero
    for number, value in enumerate(sums):
        packed = jnp.where(position == number, jnp.sum(value, axis=1, keepdims=True), packed)
    own_sums[...] = packed
    sum_copies = []
    number = 0
    for step in range(bands):
        for turn_by in range(ranks):
            if step == 0 and turn_by == 0:
                continue
            copy = remote(
                own_sums,
                all_sums.at[band, rank],
                sum_send.at[step, turn_by],
                sum_recv.at[step, turn_by],
                {"band": (band + step) % bands, "fft": (rank + turn_by) % ranks},
            )
            copy.start()
            sum_copies.append(copy)
    all_sums[band, rank] = packed
    for copy in sum_copies:
        copy.wait()
    total = zero
    for one_band in range(bands):
        for one_rank in range(ranks):
            total = total + all_sums[one_band, one_rank]
    total = jnp.broadcast_to(jnp.sum(total, axis=0, keepdims=True), (8, lanes))
    volume = float(lanes // 2) * float(rows) * float(planes * ranks)
    matrix = [[None] * bands for _ in range(bands)]
    for number, (i, l) in enumerate(entries):
        values = [
            jnp.broadcast_to(
                jnp.sum(jnp.where(position == 2 * number + half, total, 0.0), axis=1, keepdims=True),
                (8, lanes),
            )
            / volume
            for half in range(2)
        ]
        matrix[i][l] = (values[0], values[1])
    inverse = small_factor_inverse(matrix)
    back_copies = []

    def spread(value):
        return value[:1]

    for l in range(bands):

        def combine(plane, carry):
            sum_straight = jnp.zeros((rows, lanes), jnp.float32)
            sum_turned = jnp.zeros((rows, lanes), jnp.float32)
            for m in range(l + 1):
                block = potential_parts[m, plane]
                real, imag = inverse[l][m]
                sum_straight = sum_straight + spread(real) * block
                sum_turned = sum_turned + spread(imag) * block
            projector_parts[l, plane] = sum_straight + turn(sum_turned)
            return carry

        lax.fori_loop(0, piece, combine, 0)

    for chunk in turns[1:-1] + turns[:1]:
        remote(
            projector_parts.at[chunk],
            projector.at[span(band)],
            back_send.at[chunk],
            back_recv.at[band],
            {"band": chunk},
        ).start()
    projector[span(band)] = projector_parts[band]
    for chunk in turns[:-1]:
        back = remote(
            projector_parts.at[chunk],
            projector.at[span(chunk)],
            back_send.at[chunk],
            back_recv.at[chunk],
            {"band": chunk},
        )
        back.wait_recv()
        back.wait_send()
        part_copy(chunk).wait_send()
    for chunk in turns:
        far_copy(chunk).wait_send()
    near_copy(0, beside).wait_send()
    near_copy(1, beside_across).wait_send()
    to_across.wait_send()
    to_beside.wait_send()
    onward.wait_send()
    for distance in range(bands):
        for chunk in range(bands):
            for upward in (True, False):
                if distance < bands - 1:

                    @pl.when(both(has_source(upward, distance), has_next(upward)))
                    def _():
                        chain_copy(upward, distance, chunk).wait_send()

                if distance > 0 or upward:

                    @pl.when(has_source(upward, distance))
                    def _():
                        deliver(upward, distance, chunk, "wait")


def exchange(bands, ranks, orbital, partner, shift_table, shift_index):
    planes, rows, lanes = orbital.shape
    piece = planes // bands
    vmem = pl.BlockSpec(memory_space=pltpu.VMEM)
    smem = pl.BlockSpec(memory_space=pltpu.SMEM)
    out = jax.ShapeDtypeStruct((planes, rows, lanes), jnp.float32)
    grid = pltpu.VMEM((ranks * planes, rows, lanes), jnp.float32)
    held = pltpu.VMEM((bands - 1, bands, piece, rows, lanes), jnp.float32)
    quarters = pltpu.VMEM((bands, piece, rows, lanes), jnp.float32)
    dma = pltpu.SemaphoreType.DMA
    tables = [
        jnp.asarray(table)
        for table in (
            right_table(rows, -1.0),
            right_table(rows, 1.0),
            left_table(rows, -1.0),
            left_table(rows, 1.0),
        )
    ]
    return pl.pallas_call(
        functools.partial(exchange_kernel, bands, ranks),
        name="exchange",
        out_shape=(out, out),
        in_specs=[smem, smem] + [pl.BlockSpec(memory_space=pl.ANY)] * 6,
        out_specs=(vmem, vmem),
        scratch_shapes=[
            grid,
            grid,
            quarters,
            held,
            held,
            grid,
            grid,
            pltpu.VMEM((2, planes, rows, lanes), jnp.float32),
            quarters,
            quarters,
            quarters,
            quarters,
            pltpu.VMEM((8, lanes), jnp.float32),
            pltpu.VMEM((bands, ranks, 8, lanes), jnp.float32),
            dma((2, bands, bands)),
            dma((2, bands, bands)),
            dma((2, bands, bands)),
            dma((ranks, bands)),
            dma((3,)),
            dma((3,)),
            dma((bands,)),
            dma((bands,)),
            dma((bands + 2,)),
            dma((2,)),
            dma((2,)),
            dma((bands,)),
            dma((bands,)),
            dma((bands,)),
            dma((bands,)),
            dma((bands, ranks)),
            dma((bands, ranks)),
            dma((bands,)),
            dma((bands,)),
            pltpu.VMEM(orbital.shape, jnp.float32),
            pltpu.VMEM(orbital.shape, jnp.float32),
        ]
        + [pltpu.VMEM(table.shape, table.dtype) for table in tables]
        + [dma((6,))],
        compiler_params=pltpu.CompilerParams(
            collective_id=0, has_side_effects=True, vmem_limit_bytes=60 * 1024 * 1024
        ),
    )(shift_table, shift_index, orbital, partner, *tables)


def paired_body(bands, ranks, orbitals, partners, shift_table, shift_index):
    potential, projector = exchange(
        bands, ranks, orbitals[0], partners[0], shift_table, shift_index
    )
    return (potential[None], projector[None])


def body(orbitals, partners, shift_table, shift_index):
    bands = lax.axis_size("band")
    ranks = lax.axis_size("fft")
    count, planes, rows, lanes = orbitals.shape
    grid_bytes = ranks * planes * rows * lanes * 4
    paired = (
        count == 1
        and ranks == 4
        and bands == ranks
        and planes % bands == 0
        and planes % GROUP == 0
        and GROUP % (planes // bands) == 0
        and lanes == 2 * rows
        and lanes == 128
        and grid_bytes <= 2 * 1024 * 1024
    )
    if paired:
        return paired_body(bands, ranks, orbitals, partners, shift_table, shift_index)
    return general_body(orbitals, partners, shift_table, shift_index)


def solution(mesh):
    in_specs = (
        P(("kgrp", "band"), "fft", None, None),
        P(("kgrp", "band"), "fft", None, None),
        P(),
        P("kgrp"),
    )
    out_specs = (P(("kgrp", "band"), "fft", None, None), P(("kgrp", "band"), "fft", None, None))
    return jax.shard_map(body, mesh=mesh, in_specs=in_specs, out_specs=out_specs, check_vma=False)
```

profile of v0, /device:TPU:15, one launch (start us, length us, event | category | flops | bytes accessed | tf_op | source)
XLA Modules:
  0.0 97.7 jit_solution(8624981783102014120)
XLA Ops:
  0.6 0.0 copy-start.1
  0.6 0.7 copy-done.1
  1.3 0.7 copy.10.shift_table
  2.0 93.0 %exchange.1 = (f32[16,64,128]{2,1,0:T(8,128)}, f32[16,64,128]{2,1,0:T(8,128)}) custom-call(f32[8,3]{1,0:T(8,128)} %copy.10.shift_table, s32[4]{0:T(128)} %shift_index.1, f32[16,64,128]{2,1,0:T(8,128)} %bitcast.4, f32[16,64,128]{2,1,0:T(8,128)} %bitcast.5, bf16[256,256]{1,0:T(8,128)(2,1)} %constant.8.clone.right_forward_home, ...), custom_call_target="tpu_custom_call" | custom-call | tf_op jit(solution)/shard_map/exchange/pallas_call | solution.py:860
  95.0 0.0 copy-start
  95.0 1.9 %copy.13 = f32[1,16,64,128]{3,2,1,0:T(8,128)} copy(f32[1,16,64,128]{3,2,1,0:T(8,128)} %bitcast.7) | data formatting | bytes 1048576
  96.9 0.0 copy-done
  96.9 0.8 copy.14
Async XLA Ops:
  0.6 0.7 copy-start.1
  95.0 2.0 %copy-start = (f32[16,64,128]{2,1,0:T(8,128)S(1)}, f32[16,64,128]{2,1,0:T(8,128)}, u32[]{:S(2)}) copy-start(f32[16,64,128]{2,1,0:T(8,128)} %get-tuple-element.5) | copy-start | bytes 1572868
where the time goes:
time: 97.9 us; the launch traced here: 97.7 us
  Pallas kernels  93 us (95%)
  local copies, waits for them, and re-layouts  4.09 us (4%)
    pallas_call x1, Pallas kernels, exchange(): pl.pallas_call(functools.partial(exchange_kernel, bands, ranks), name='ex...  93 us
    unnamed x7, local copies, waits for them, and re-layouts  4.09 us

commit v1 on v0

--- a/solution.py
+++ b/solution.py
@@ -412,51 +412,87 @@
     projector,
     orbital_grid,
     partner_grid,
-    orbital_parts,
-    from_below,
-    from_above,
     work,
     partial,
+    partner,
+    detour,
     near,
     outgoing,
     arriving,
-    potential_parts,
-    projector_parts,
+    passed,
+    others,
+    tallies,
     own_sums,
     all_sums,
-    chain_send,
-    chain_recv,
-    deliver_send,
-    deliver_recv,
-    grid_send,
-    grid_recv,
-    early_send,
-    early_recv,
-    local_sem,
-    near_send,
-    near_recv,
-    far_send,
-    far_recv,
-    part_send,
-    part_recv,
-    sum_send,
-    sum_recv,
-    back_send,
-    back_recv,
-    orbital,
-    partner,
     right_forward,
     right_inverse,
     left_forward,
     left_inverse,
     load_sem,
+    gather_send,
+    detour_send,
+    detour_recv,
+    onward_send,
+    chain_send,
+    partner_recv,
+    grid_send,
+    grid_recv,
+    other_send,
+    other_recv,
+    near_send,
+    near_recv,
+    far_send,
+    far_recv,
+    up_send,
+    up_recv,
+    sum_send,
+    sum_recv,
 ):
-    loads = [
-        pltpu.make_async_copy(home, here, load_sem.at[number])
-        for number, (home, here) in enumerate(
+    planes, rows, lanes = potential.shape
+    chunks = bands
+    piece = planes // chunks
+    per_group = GROUP // piece
+    halves_count = planes // GROUP
+    last = bands - 1
+    direct = chunks // 2
+    band = lax.axis_index("band")
+    rank = lax.axis_index("fft")
+    beside = rank + 1 - 2 * (rank % 2)
+    across = (rank + 2) % ranks
+    beside_across = (beside + 2) % ranks
+    slabs = (rank, beside, across, beside_across)
+    home = 2 * (rank % 2) + (rank // 2 + rank % 2) % 2
+    keeper = 2 * ((band // 2 + band % 2) % 2) + band // 2
+
+    def both(*conditions):
+        return functools.reduce(jnp.logical_and, conditions)
+
+    def either(*conditions):
+        return functools.reduce(jnp.logical_or, conditions)
+
+    at_home = band == home
+    at_end = either(band == 0, band == last)
+    early = either(at_home, band == 1, band == last - 1)
+    low_side = rank < ranks // 2
+    takes_detour = both(at_end, low_side)
+    gives_detour = both(jnp.logical_not(at_end), low_side)
+
+    def span(index):
+        return pl.ds(index * piece, piece)
+
+    def slab(index):
+        return pl.ds(index * planes, planes)
+
+    def window(index, chunk):
+        return pl.ds(index * planes + chunk * piece, piece)
+
+    own_slab = pltpu.make_async_copy(orbital_home, orbital_grid.at[slab(rank)], load_sem.at[1])
+    partner_load = pltpu.make_async_copy(partner_home, partner, load_sem.at[0])
+    home_load = pltpu.make_async_copy(partner_home, partner_grid.at[slab(rank)], load_sem.at[2])
+    table_loads = [
+        pltpu.make_async_copy(source, here, load_sem.at[3 + number])
+        for number, (source, here) in enumerate(
             (
-                (partner_home, partner),
-                (orbital_home, orbital),
                 (right_forward_home, right_forward),
                 (left_forward_home, left_forward),
                 (right_inverse_home, right_inverse),
@@ -464,14 +500,15 @@
             )
         )
     ]
-    for load in loads:
+    partner_load.start()
+
+    @pl.when(at_home)
+    def _():
+        home_load.start()
+
+    own_slab.start()
+    for load in table_loads:
         load.start()
-    band = lax.axis_index("band")
-    rank = lax.axis_index("fft")
-    planes, rows, lanes = orbital.shape
-    piece = planes // bands
-    per_group = GROUP // piece
-    halves_count = planes // GROUP
     greet(
         [
             {"band": (band + step) % bands, "fft": (rank + turn_by) % ranks}
@@ -480,183 +517,189 @@
             if step or turn_by
         ]
     )
-    loads[0].wait()
-
-    def span(index):
-        return pl.ds(index * piece, piece)
-
-    def slab(index):
-        return pl.ds(index * planes, planes)
-
-    beside = rank + 1 - 2 * (rank % 2)
-    across = (rank + 2) % ranks
-    beside_across = (beside + 2) % ranks
-
-    def chain_copy(upward, distance, chunk):
-        held = from_below if upward else from_above
-        source = partner.at[span(chunk)] if distance == 0 else held.at[distance - 1, chunk]
-        way = 0 if upward else 1
+
+    def gather_copy(chunk):
+        return remote(
+            partner.at[span(chunk)],
+            partner_grid.at[window(rank, chunk)],
+            gather_send.at[chunk],
+            partner_recv.at[rank, chunk],
+            {"fft": keeper},
+        )
+
+    def detour_copy(chunk):
+        return remote(
+            partner.at[span(chunk)],
+            detour.at[chunk],
+            detour_send.at[chunk],
+            detour_recv.at[chunk],
+            {"band": last * (band - 1)},
+        )
+
+    def onward_copy(chunk):
+        return remote(
+            detour.at[chunk],
+            partner_grid.at[window(rank, chunk)],
+            onward_send.at[chunk],
+            partner_recv.at[rank, chunk],
+            {"fft": ranks // 2 + band // last},
+        )
+
+    def chain_copy(way, turn_to, chunk):
+        place = partner_grid.at[window(slabs[turn_to], chunk)]
+        return remote(
+            place,
+            place,
+            chain_send.at[way, turn_to, chunk],
+            partner_recv.at[slabs[turn_to], chunk],
+            {"band": band + 1 - 2 * way},
+        )
+
+    def passes(way, turn_to):
+        if way == 0:
+            go = both(band >= home, band < last)
+            short = both(band == last - 1, rank == ranks - 1)
+        else:
+            go = both(band <= home, band > 0)
+            short = both(band == 1, rank == ranks // 2)
+        return both(go, jnp.logical_not(short)) if turn_to > 1 else go
+
+    def arrive(turn_to, chunk):
+        def wait():
+            chain_copy(0, turn_to, chunk).wait_recv()
+
+        if turn_to:
+            wait()
+        else:
+            pl.when(jnp.logical_not(at_home))(wait)
+
+    def step(turn_to, chunk):
+        arrive(turn_to, chunk)
+        for way in (0, 1):
+
+            @pl.when(passes(way, turn_to))
+            def _():
+                chain_copy(way, turn_to, chunk).start()
+
+    tail = [(turn_to, half) for half in range(halves_count) for turn_to in (2, 3)]
+
+    def of_half(half):
+        return range(half * per_group, (half + 1) * per_group)
+
+    partner_load.wait()
+    for chunk in range(chunks):
+
+        @pl.when(jnp.logical_not(at_home))
+        def _():
+            gather_copy(chunk).start()
+
+        @pl.when(gives_detour)
+        def _():
+            detour_copy(chunk).start()
+
+    @pl.when(at_home)
+    def _():
+        home_load.wait()
+
+    own_slab.wait()
+    own_orbital = orbital_grid.at[slab(rank)]
+    to_across = remote(own_orbital, own_orbital, grid_send.at[0], grid_recv.at[0], {"fft": across})
+    to_beside = remote(own_orbital, own_orbital, grid_send.at[1], grid_recv.at[1], {"fft": beside})
+    other_orbital = orbital_grid.at[slab(across)]
+    onward = remote(
+        other_orbital, other_orbital, grid_send.at[2], grid_recv.at[2], {"fft": beside}
+    )
+    to_across.start()
+    to_beside.start()
+
+    def take_detour(condition, chunk):
+        @pl.when(both(takes_detour, condition))
+        def _():
+            detour_copy(chunk).wait_recv()
+            onward_copy(chunk).start()
+
+    for turn_to in (0, 1):
+        for chunk in range(chunks):
+            step(turn_to, chunk)
+            if turn_to == 1:
+                take_detour(jnp.logical_not(at_home), chunk)
+
+    def other_copy(which, slot, where, source=own_orbital):
         return remote(
             source,
-            held.at[distance, chunk],
-            chain_send.at[way, distance, chunk],
-            chain_recv.at[way, distance, chunk],
-            {"band": band + 1 if upward else band - 1},
-        )
-
-    def deliver(upward, distance, chunk, act):
-        held = from_below if upward else from_above
-        source = partner.at[span(chunk)] if distance == 0 else held.at[distance - 1, chunk]
-        owner = band - distance if upward else band + distance
-        target = partner_grid.at[pl.ds(rank * planes + chunk * piece, piece)]
-        way = 0 if upward else 1
-
-        @pl.when(owner == rank)
+            others.at[slot],
+            other_send.at[which],
+            other_recv.at[slot],
+            {"band": where},
+        )
+
+    @pl.when(early)
+    def _():
+        for turn_to, half in tail:
+            for chunk in of_half(half):
+                if turn_to == 2:
+                    take_detour(at_home, chunk)
+            for chunk in of_half(half):
+                step(turn_to, chunk)
+
+    @pl.when(band == 0)
+    def _():
+        other_copy(0, 0, 1).start()
+
+    @pl.when(band == last)
+    def _():
+        other_copy(0, 1, last - 1).start()
+
+    to_across.wait_recv()
+    onward.start()
+    for load in table_loads:
+        load.wait()
+    to_beside.wait_recv()
+    onward.wait_recv()
+
+    def forward(group):
+        forward_group(group, orbital_grid, partner_grid, work, right_forward, left_forward)
+
+    def forward_near(index, carry):
+        forward(
+            (rank + index // halves_count * (beside - rank)) * halves_count + index % halves_count
+        )
+        return carry
+
+    lax.fori_loop(0, 2 * halves_count, forward_near, 0)
+    for turn_to, half in tail:
+
+        @pl.when(jnp.logical_not(early))
         def _():
-            if act == "start":
-                pltpu.make_async_copy(source, target, local_sem.at[chunk]).start()
-
-        @pl.when(owner != rank)
-        def _():
-            copy = remote(
-                source,
-                target,
-                deliver_send.at[way, distance, chunk],
-                deliver_recv.at[rank, chunk],
-                {"fft": owner},
-            )
-            copy.start() if act == "start" else copy.wait_send()
-
-    def has_source(upward, distance):
-        return band >= distance if upward else band + distance <= bands - 1
-
-    def has_next(upward):
-        return band <= bands - 2 if upward else band >= 1
-
-    def both(first, second):
-        return jnp.logical_and(first, second)
-
-    def forward_half(half):
-        for chunk in range(half * per_group, (half + 1) * per_group):
-            target = partner_grid.at[pl.ds(rank * planes + chunk * piece, piece)]
-            pltpu.make_async_copy(partner.at[span(chunk)], target, local_sem.at[chunk]).wait()
-            for step in range(1, ranks):
-                source = (rank + step) % ranks
-                target = partner_grid.at[pl.ds(source * planes + chunk * piece, piece)]
-                remote(
-                    target,
-                    target,
-                    deliver_send.at[0, 0, chunk],
-                    deliver_recv.at[source, chunk],
-                    {"fft": source},
-                ).wait_recv()
-
-        def forward(index, carry):
-            forward_group(
-                index * halves_count + half,
-                orbital_grid,
-                partner_grid,
-                work,
-                right_forward,
-                left_forward,
-            )
-            return carry
-
-        lax.fori_loop(0, ranks, forward, 0)
-
-    for chunk in range(bands):
-        for upward in (True, False):
-
-            @pl.when(has_next(upward))
-            def _():
-                chain_copy(upward, 0, chunk).start()
-
-    loads[1].wait()
-    to_across = remote(
-        orbital, orbital_grid.at[slab(rank)], grid_send.at[0], grid_recv.at[0], {"fft": across}
-    )
-    to_beside = remote(
-        orbital, orbital_grid.at[slab(rank)], grid_send.at[1], grid_recv.at[1], {"fft": beside}
-    )
-    to_across.start()
-    to_beside.start()
-    own_grid = pltpu.make_async_copy(orbital, orbital_grid.at[slab(rank)], local_sem.at[bands])
-    own_grid.start()
-    for chunk in range(bands):
-        deliver(True, 0, chunk, "start")
-    onward = remote(
-        orbital_grid.at[slab(across)],
-        orbital_grid.at[slab(across)],
-        grid_send.at[2],
-        grid_recv.at[2],
-        {"fft": beside},
-    )
-    for distance in range(1, bands):
-        for chunk in range(bands):
-            for upward in (True, False):
-
-                @pl.when(has_source(upward, distance))
-                def _():
-                    chain_copy(upward, distance - 1, chunk).wait_recv()
-
-                if distance < bands - 1:
-
-                    @pl.when(both(has_source(upward, distance), has_next(upward)))
-                    def _():
-                        chain_copy(upward, distance, chunk).start()
-
-                @pl.when(has_source(upward, distance))
-                def _():
-                    deliver(upward, distance, chunk, "start")
-
-            if distance == bands - 1 and chunk > 0 and chunk % per_group == 0:
-                forward_half(chunk // per_group - 1)
-
-        if distance == 1:
-            to_across.wait_recv()
-            onward.start()
-            own_grid.wait()
-            for load in loads[2:]:
-                load.wait()
-            to_beside.wait_recv()
-            onward.wait_recv()
-    forward_half(halves_count - 1)
-    early_copies = []
-    for step in range(1, bands):
-        other = (band + step) % bands
-        copy = remote(
-            orbital.at[span(other)],
-            orbital_parts.at[band],
-            early_send.at[step - 1],
-            early_recv.at[step - 1],
-            {"band": other},
-        )
-        copy.start()
-        early_copies.append(copy)
-    own_part = pltpu.make_async_copy(
-        orbital.at[span(band)], orbital_parts.at[band], local_sem.at[bands + 1]
-    )
-    own_part.start()
-
-    chosen = shift_index[rank]
-    shift = [shift_table[chosen, axis] for axis in range(3)]
+            for chunk in of_half(half):
+                arrive(turn_to, chunk)
+
+        forward(slabs[turn_to] * halves_count + half)
+
+    chosen = shift_index[home]
+    shift = [shift_table[axis, chosen] for axis in range(3)]
     middle_pairs(shift, work, left_forward, left_inverse)
 
-    def backward_slab(index):
-        def backward(half, carry):
-            backward_group(
-                index * halves_count + half, partner_grid, partial, work, right_inverse, left_inverse
-            )
-            return carry
-
-        lax.fori_loop(0, halves_count, backward, 0)
-
-    def near_copy(which, index):
+    @pl.when(band == last)
+    def _():
+        other_copy(1, 1, 0).start()
+
+    @pl.when(band == 1)
+    def _():
+        other_copy(0, 0, 0).wait_recv()
+        other_copy(0, 0, 2, others.at[0]).start()
+
+    def backward(index, half):
+        backward_group(
+            index * halves_count + half, partner_grid, partial, work, right_inverse, left_inverse
+        )
+
+    def near_copy(which, index, half):
         return remote(
-            partial.at[slab(index)],
-            near.at[which],
-            near_send.at[which],
-            near_recv.at[which],
+            partial.at[pl.ds(index * planes + half * GROUP, GROUP)],
+            near.at[which, pl.ds(half * GROUP, GROUP)],
+            near_send.at[which, half],
+            near_recv.at[which, half],
             {"fft": beside},
         )
 
@@ -669,92 +712,147 @@
             {"fft": across},
         )
 
-    def window(index, chunk):
-        return pl.ds(index * planes + chunk * piece, piece)
-
-    turns = [(band + step) % bands for step in range(1, bands + 1)]
-    backward_slab(beside_across)
-    near_copy(1, beside_across).start()
-    backward_slab(across)
-    near_copy(1, beside_across).wait_recv()
-    for chunk in turns:
-        outgoing[chunk] = partial[window(across, chunk)] + near[1, span(chunk)]
-        far_copy(chunk).start()
-    backward_slab(beside)
-    near_copy(0, beside).start()
-    backward_slab(rank)
-    near_copy(0, beside).wait_recv()
-
-    def part_copy(chunk):
+    def up_copy(owner, chunk, own=False):
+        held = passed.at[owner, span(chunk)]
         return remote(
-            potential.at[span(chunk)],
-            potential_parts.at[band],
-            part_send.at[chunk],
-            part_recv.at[band],
-            {"band": chunk},
-        )
-
-    for step, chunk in enumerate(turns):
+            potential.at[span(chunk)] if own else held,
+            held,
+            up_send.at[owner, chunk],
+            up_recv.at[owner, chunk],
+            {"band": band + 1},
+        )
+
+    for half in range(halves_count):
+        backward(beside_across, half)
+        near_copy(1, beside_across, half).start()
+        backward(across, half)
+        near_copy(1, beside_across, half).wait_recv()
+        for chunk in of_half(half):
+            outgoing[chunk] = partial[window(across, chunk)] + near[1, span(chunk)]
+            far_copy(chunk).start()
+    for half in range(halves_count):
+        backward(beside, half)
+        near_copy(0, beside, half).start()
+    for half in range(halves_count):
+        backward(rank, half)
+
+    zero = jnp.zeros((8, lanes), jnp.float32)
+    for number in range(tallies.shape[0]):
+        tallies[number] = zero
+
+    def inner(slot, left, right, chunk):
+        def accumulate(plane, sums):
+            straight = right(plane)
+            value = left(plane)
+            return tuple(
+                running + jnp.sum((value * other).reshape(rows // 8, 8, lanes), axis=0)
+                for running, other in zip(sums, (straight, turn(straight)))
+            )
+
+        sums = lax.fori_loop(
+            chunk * piece,
+            (chunk + 1) * piece,
+            accumulate,
+            (tallies[2 * slot], tallies[2 * slot + 1]),
+        )
+        tallies[2 * slot] = sums[0]
+        tallies[2 * slot + 1] = sums[1]
+
+    def own_potential(plane):
+        return potential[plane]
+
+    def own_values(plane):
+        return orbital_grid[rank * planes + plane]
+
+    holds_first = either(band == 1, band == 2)
+    holds_last = either(band == 0, band == 2)
+
+    def with_others(span_of_chunks, wait):
+        for slot, held in ((0, holds_first), (1, holds_last)):
+
+            @pl.when(held)
+            def _():
+                if wait and slot:
+                    other_copy(0, 1, 0).wait_recv()
+                for chunk in span_of_chunks:
+                    inner(1 + slot, lambda plane: others[slot, plane], own_potential, chunk)
+
+    for chunk in range(chunks):
+        if chunk % per_group == 0:
+            near_copy(0, beside, chunk // per_group).wait_recv()
         far_copy(chunk).wait_recv()
         potential[span(chunk)] = (
             partial[window(rank, chunk)] + near[0, span(chunk)]
         ) + arriving[chunk]
-        if step < bands - 1:
-            part_copy(chunk).start()
-        else:
-            potential_parts[band] = potential[span(band)]
-    for chunk in turns[:-1]:
-        remote(
-            potential_parts.at[chunk],
-            potential_parts.at[chunk],
-            part_send.at[chunk],
-            part_recv.at[chunk],
-            {"band": chunk},
-        ).wait_recv()
-    for copy in early_copies:
-        copy.wait()
-    own_part.wait()
+
+        @pl.when(band < last - 1 if chunk >= direct else band < last)
+        def _():
+            up_copy(band, chunk, True).start()
+
+        inner(0, own_values, own_potential, chunk)
+        if chunk == chunks - 2:
+
+            @pl.when(band == 2)
+            def _():
+                other_copy(0, 0, 0).wait_recv()
+
+            with_others(range(chunk + 1), True)
+    with_others([chunks - 1], False)
+
+    @pl.when(band == 2)
+    def _():
+        for chunk in range(chunks):
+            up_copy(1, chunk).wait_recv()
+            if chunk < direct:
+                up_copy(1, chunk).start()
+            inner(3, own_values, lambda plane: passed[1, plane], chunk)
+            inner(4, lambda plane: others[1, plane], lambda plane: passed[1, plane], chunk)
 
     entries = [(i, l) for i in range(bands) for l in range(i + 1)]
+    row_start = band * (band + 1) // 2
+    places = (
+        row_start + band,
+        row_start,
+        entries.index((last, 0)) + band,
+        entries.index((2, 1)),
+        entries.index((last, 1)),
+    )
     position = lax.broadcasted_iota(jnp.int32, (8, lanes), 1)
-
-    def accumulate(plane, sums):
-        turned = []
-        straight = []
-        for l in range(bands):
-            block = potential_parts[l, plane]
-            straight.append(block)
-            turned.append(turn(block))
-        result = []
-        for number, (i, l) in enumerate(entries):
-            left = orbital_parts[i, plane]
-            for half, right in enumerate((straight[l], turned[l])):
-                product = (left * right).reshape(rows // 8, 8, lanes)
-                result.append(sums[2 * number + half] + jnp.sum(product, axis=0))
-        return tuple(result)
-
-    zero = jnp.zeros((8, lanes), jnp.float32)
-    sums = lax.fori_loop(0, piece, accumulate, (zero,) * (2 * len(entries)))
     packed = zero
-    for number, value in enumerate(sums):
-        packed = jnp.where(position == number, jnp.sum(value, axis=1, keepdims=True), packed)
+    for slot, place in enumerate(places):
+        for half in range(2):
+            value = jnp.sum(tallies[2 * slot + half], axis=1, keepdims=True)
+            value = -value if (slot, half) == (1, 1) else value
+            packed = packed + jnp.where(position == 2 * place + half, value, 0.0)
     own_sums[...] = packed
     sum_copies = []
-    number = 0
-    for step in range(bands):
+    for step_by in range(bands):
         for turn_by in range(ranks):
-            if step == 0 and turn_by == 0:
+            if step_by == 0 and turn_by == 0:
                 continue
             copy = remote(
                 own_sums,
                 all_sums.at[band, rank],
-                sum_send.at[step, turn_by],
-                sum_recv.at[step, turn_by],
-                {"band": (band + step) % bands, "fft": (rank + turn_by) % ranks},
+                sum_send.at[step_by, turn_by],
+                sum_recv.at[step_by, turn_by],
+                {"band": (band + step_by) % bands, "fft": (rank + turn_by) % ranks},
             )
             copy.start()
             sum_copies.append(copy)
     all_sums[band, rank] = packed
+
+    @pl.when(either(band == 1, band == 2))
+    def _():
+        for chunk in range(direct):
+            up_copy(0, chunk).wait_recv()
+            up_copy(0, chunk).start()
+
+    @pl.when(band == 1)
+    def _():
+        for chunk in range(direct, chunks):
+            up_copy(0, chunk).wait_recv()
+            up_copy(0, chunk).start()
+
     for copy in sum_copies:
         copy.wait()
     total = zero
@@ -775,78 +873,125 @@
         ]
         matrix[i][l] = (values[0], values[1])
     inverse = small_factor_inverse(matrix)
-    back_copies = []
-
-    def spread(value):
-        return value[:1]
-
-    for l in range(bands):
-
-        def combine(plane, carry):
+
+    def combine(row, own, members, start, stop, put):
+        def one_plane(plane, carry):
             sum_straight = jnp.zeros((rows, lanes), jnp.float32)
             sum_turned = jnp.zeros((rows, lanes), jnp.float32)
-            for m in range(l + 1):
-                block = potential_parts[m, plane]
-                real, imag = inverse[l][m]
-                sum_straight = sum_straight + spread(real) * block
-                sum_turned = sum_turned + spread(imag) * block
-            projector_parts[l, plane] = sum_straight + turn(sum_turned)
+            for m in members:
+                block = potential[plane] if m is None else passed[m, plane]
+                real, imag = inverse[row][own if m is None else m]
+                sum_straight = sum_straight + real[:1] * block
+                sum_turned = sum_turned + imag[:1] * block
+            put(plane, sum_straight + turn(sum_turned))
             return carry
 
-        lax.fori_loop(0, piece, combine, 0)
-
-    for chunk in turns[1:-1] + turns[:1]:
-        remote(
-            projector_parts.at[chunk],
-            projector.at[span(band)],
-            back_send.at[chunk],
-            back_recv.at[band],
-            {"band": chunk},
-        ).start()
-    projector[span(band)] = projector_parts[band]
-    for chunk in turns[:-1]:
-        back = remote(
-            projector_parts.at[chunk],
-            projector.at[span(chunk)],
-            back_send.at[chunk],
-            back_recv.at[chunk],
-            {"band": chunk},
-        )
-        back.wait_recv()
-        back.wait_send()
-        part_copy(chunk).wait_send()
-    for chunk in turns:
+        lax.fori_loop(start, stop, one_plane, 0)
+
+    def put_whole(plane, value):
+        projector[plane] = value
+
+    def put_more(plane, value):
+        projector[plane] = projector[plane] + value
+
+    def put_lifted(plane, value):
+        passed[2, plane] = value
+
+    for row in range(2):
+
+        @pl.when(band == row)
+        def _():
+            combine(row, row, [None, 0][: row + 1], 0, planes, put_whole)
+
+    @pl.when(band == 2)
+    def _():
+        for chunk in range(direct, chunks):
+            up_copy(0, chunk).wait_recv()
+            combine(last, 2, (0, 1, None), chunk * piece, (chunk + 1) * piece, put_lifted)
+            up_copy(2, chunk).start()
+        combine(2, 2, (0, 1, None), 0, planes, put_whole)
+
+    @pl.when(band == last)
+    def _():
+        for member in (2, 1):
+            for chunk in range(direct):
+                up_copy(member, chunk).wait_recv()
+        combine(last, last, (1, 2, None), 0, direct * piece, put_whole)
+        combine(last, last, (None,), direct * piece, planes, put_whole)
+        for chunk in range(direct):
+            up_copy(0, chunk).wait_recv()
+            combine(last, last, (0,), chunk * piece, (chunk + 1) * piece, put_more)
+        for chunk in range(direct, chunks):
+            up_copy(2, chunk).wait_recv()
+            projector[span(chunk)] = projector[span(chunk)] + passed[2, span(chunk)]
+
+    for chunk in range(chunks):
+
+        @pl.when(jnp.logical_not(at_home))
+        def _():
+            gather_copy(chunk).wait_send()
+
+        @pl.when(gives_detour)
+        def _():
+            detour_copy(chunk).wait_send()
+
+        @pl.when(takes_detour)
+        def _():
+            onward_copy(chunk).wait_send()
+
+        for turn_to in range(len(slabs)):
+            for way in (0, 1):
+
+                @pl.when(passes(way, turn_to))
+                def _():
+                    chain_copy(way, turn_to, chunk).wait_send()
+
         far_copy(chunk).wait_send()
-    near_copy(0, beside).wait_send()
-    near_copy(1, beside_across).wait_send()
+
+        @pl.when(band < last)
+        def _():
+            up_copy(band, chunk, True).wait_send()
+
+        if chunk < direct:
+
+            @pl.when(band == 2)
+            def _():
+                up_copy(1, chunk).wait_send()
+
+        @pl.when(band == 1 if chunk >= direct else either(band == 1, band == 2))
+        def _():
+            up_copy(0, chunk).wait_send()
+
+    @pl.when(band != 2)
+    def _():
+        other_copy(0, 0, 1).wait_send()
+
+    @pl.when(band == last)
+    def _():
+        other_copy(1, 1, 0).wait_send()
+
+    for half in range(halves_count):
+        near_copy(0, beside, half).wait_send()
+        near_copy(1, beside_across, half).wait_send()
     to_across.wait_send()
     to_beside.wait_send()
     onward.wait_send()
-    for distance in range(bands):
-        for chunk in range(bands):
-            for upward in (True, False):
-                if distance < bands - 1:
-
-                    @pl.when(both(has_source(upward, distance), has_next(upward)))
-                    def _():
-                        chain_copy(upward, distance, chunk).wait_send()
-
-                if distance > 0 or upward:
-
-                    @pl.when(has_source(upward, distance))
-                    def _():
-                        deliver(upward, distance, chunk, "wait")
 
 
 def exchange(bands, ranks, orbital, partner, shift_table, shift_index):
     planes, rows, lanes = orbital.shape
-    piece = planes // bands
+    chunks = bands
+    halves_count = planes // GROUP
     vmem = pl.BlockSpec(memory_space=pltpu.VMEM)
     smem = pl.BlockSpec(memory_space=pltpu.SMEM)
     out = jax.ShapeDtypeStruct((planes, rows, lanes), jnp.float32)
     grid = pltpu.VMEM((ranks * planes, rows, lanes), jnp.float32)
-    held = pltpu.VMEM((bands - 1, bands, piece, rows, lanes), jnp.float32)
-    quarters = pltpu.VMEM((bands, piece, rows, lanes), jnp.float32)
+    slab = pltpu.VMEM((planes, rows, lanes), jnp.float32)
+    quarters = pltpu.VMEM((chunks, planes // chunks, rows, lanes), jnp.float32)
+
+    def slab_list(count):
+        return pltpu.VMEM((count, planes, rows, lanes), jnp.float32)
+
     dma = pltpu.SemaphoreType.DMA
     tables = [
         jnp.asarray(table)
@@ -866,46 +1011,45 @@
         scratch_shapes=[
             grid,
             grid,
-            quarters,
-            held,
-            held,
             grid,
             grid,
-            pltpu.VMEM((2, planes, rows, lanes), jnp.float32),
+            slab,
+            quarters,
+            slab_list(2),
             quarters,
             quarters,
-            quarters,
-            quarters,
+            slab_list(bands - 1),
+            slab_list(2),
+            pltpu.VMEM((10, 8, lanes), jnp.float32),
             pltpu.VMEM((8, lanes), jnp.float32),
             pltpu.VMEM((bands, ranks, 8, lanes), jnp.float32),
-            dma((2, bands, bands)),
-            dma((2, bands, bands)),
-            dma((2, bands, bands)),
-            dma((ranks, bands)),
+        ]
+        + [pltpu.VMEM(table.shape, table.dtype) for table in tables]
+        + [
+            dma((7,)),
+            dma((chunks,)),
+            dma((chunks,)),
+            dma((chunks,)),
+            dma((chunks,)),
+            dma((2, ranks, chunks)),
+            dma((ranks, chunks)),
             dma((3,)),
             dma((3,)),
-            dma((bands,)),
-            dma((bands,)),
-            dma((bands + 2,)),
             dma((2,)),
             dma((2,)),
-            dma((bands,)),
-            dma((bands,)),
-            dma((bands,)),
-            dma((bands,)),
+            dma((2, halves_count)),
+            dma((2, halves_count)),
+            dma((chunks,)),
+            dma((chunks,)),
+            dma((bands, chunks)),
+            dma((bands, chunks)),
             dma((bands, ranks)),
             dma((bands, ranks)),
-            dma((bands,)),
-            dma((bands,)),
-            pltpu.VMEM(orbital.shape, jnp.float32),
-            pltpu.VMEM(orbital.shape, jnp.float32),
-        ]
-        + [pltpu.VMEM(table.shape, table.dtype) for table in tables]
-        + [dma((6,))],
+        ],
         compiler_params=pltpu.CompilerParams(
             collective_id=0, has_side_effects=True, vmem_limit_bytes=60 * 1024 * 1024
         ),
-    )(shift_table, shift_index, orbital, partner, *tables)
+    )(shift_table.T, shift_index, orbital, partner, *tables)
 
 
 def paired_body(bands, ranks, orbitals, partners, shift_table, shift_index):

time: 97.9 us -> 88 us (0.90)
  the two profiles are of different devices: /device:TPU:15 before, /device:TPU:24 now
where the time goes in v1:
time: 88 us; the launch traced here: 87.9 us
  Pallas kernels  84.5 us (96%)
  local copies, waits for them, and re-layouts  2.74 us (3%)
    pallas_call x1, Pallas kernels, exchange(): pl.pallas_call(functools.partial(exchange_kernel, bands, ranks), name='ex...  84.5 us
    unnamed x4, local copies, waits for them, and re-layouts  2.74 us

profile of v1, /device:TPU:24, one launch (start us, length us, event | category | flops | bytes accessed | tf_op | source)
XLA Modules:
  0.0 87.9 jit_solution(15959874888646341894)
XLA Ops:
  0.6 84.5 %exchange.1 = (f32[16,64,128]{2,1,0:T(8,128)}, f32[16,64,128]{2,1,0:T(8,128)}) custom-call(f32[3,8]{1,0:T(4,128)} %bitcast.9, s32[4]{0:T(128)} %shift_index.1, f32[16,64,128]{2,1,0:T(8,128)} %bitcast.7, f32[16,64,128]{2,1,0:T(8,128)} %bitcast.8, bf16[256,256]{1,0:T(8,128)(2,1)} %constant.8.clone.right_forward_home, ...), custom_call_target="tpu_custom_call" | custom-call | tf_op jit(solution)/shard_map/exchange/pallas_call | solution.py:1005
  85.1 0.0 copy-start
  85.1 1.9 %copy.12 = f32[1,16,64,128]{3,2,1,0:T(8,128)} copy(f32[1,16,64,128]{3,2,1,0:T(8,128)} %bitcast.6) | data formatting | bytes 1048576
  87.1 0.0 copy-done
  87.1 0.8 copy.13
Async XLA Ops:
  85.1 2.0 %copy-start = (f32[16,64,128]{2,1,0:T(8,128)S(1)}, f32[16,64,128]{2,1,0:T(8,128)}, u32[]{:S(2)}) copy-start(f32[16,64,128]{2,1,0:T(8,128)} %get-tuple-element.5) | copy-start | bytes 1572868

commit v2 on v1

--- a/solution.py
+++ b/solution.py
@@ -372,8 +372,8 @@
     partial[span] = (real * field - imag * turn(field)).reshape(GROUP, rows, lanes)
 
 
-def middle_pairs(shift, work, forward, inverse):
-    columns, extent, lanes = work.shape
+def fill_screen(shift, screen):
+    columns, extent, lanes = screen.shape
     first = frequency(lax.broadcasted_iota(jnp.int32, (extent, lanes), 0), extent)
     third_place = lax.broadcasted_iota(jnp.int32, (extent, lanes), 1)
     third_place = jnp.where(third_place < lanes // 2, third_place, third_place - lanes // 2)
@@ -381,20 +381,27 @@
     base = (first + shift[0]) ** 2 + (third + shift[2]) ** 2 + SCREEN_SQUARE
     scale = FOUR_PI / (float(extent) * float(columns) * float(lanes // 2))
 
+    def one_column(column, carry):
+        second = jnp.where(column < columns // 2, column, column - columns)
+        offset = (second.astype(jnp.float32) + shift[1]) ** 2
+        screen[column] = scale / (base + offset)
+        return carry
+
+    lax.fori_loop(0, columns, one_column, 0, unroll=2)
+
+
+def middle_pairs(screen, work, forward, inverse):
+    columns = work.shape[0]
+
     def one_pair(pair, carry):
         spectra = left_product(work[2 * pair], work[2 * pair + 1], forward[...])
-        scaled = []
-        for which in range(2):
-            column = 2 * pair + which
-            second = jnp.where(column < columns // 2, column, column - columns)
-            offset = (second.astype(jnp.float32) + shift[1]) ** 2
-            scaled.append(spectra[which] * (scale / (base + offset)))
+        scaled = [spectra[which] * screen[2 * pair + which] for which in range(2)]
         fields = left_product(scaled[0], scaled[1], inverse[...])
         work[2 * pair] = fields[0]
         work[2 * pair + 1] = fields[1]
         return carry
 
-    lax.fori_loop(0, columns // 2, one_pair, 0, unroll=4)
+    lax.fori_loop(0, columns // 2, one_pair, 0, unroll=16)
 
 
 def exchange_kernel(
@@ -454,7 +461,9 @@
     per_group = GROUP // piece
     halves_count = planes // GROUP
     last = bands - 1
-    direct = chunks // 2
+    cuts = 2 * chunks
+    slice_size = planes // cuts
+    direct = 4 * cuts // 8
     band = lax.axis_index("band")
     rank = lax.axis_index("fft")
     beside = rank + 1 - 2 * (rank % 2)
@@ -479,6 +488,9 @@
 
     def span(index):
         return pl.ds(index * piece, piece)
+
+    def cut_span(cut):
+        return pl.ds(cut * slice_size, slice_size)
 
     def slab(index):
         return pl.ds(index * planes, planes)
@@ -624,49 +636,68 @@
             if turn_to == 1:
                 take_detour(jnp.logical_not(at_home), chunk)
 
-    def other_copy(which, slot, where, source=own_orbital):
+    def other_copy(slot, where, source=own_orbital):
         return remote(
             source,
             others.at[slot],
-            other_send.at[which],
+            other_send.at[slot, where],
             other_recv.at[slot],
             {"band": where},
         )
 
+    def forward(group):
+        forward_group(group, orbital_grid, partner_grid, work, right_forward, left_forward)
+
+    def forward_near(index):
+        forward(
+            (rank + index // halves_count * (beside - rank)) * halves_count + index % halves_count
+        )
+
+    for load in table_loads:
+        load.wait()
+    to_beside.wait_recv()
+
     @pl.when(early)
     def _():
-        for turn_to, half in tail:
+        for number, (turn_to, half) in enumerate(tail):
             for chunk in of_half(half):
                 if turn_to == 2:
                     take_detour(at_home, chunk)
+            if number == len(tail) - 1:
+
+                @pl.when(jnp.logical_not(at_home))
+                def _():
+                    to_across.wait_recv()
+                    onward.start()
+
             for chunk in of_half(half):
                 step(turn_to, chunk)
-
-    @pl.when(band == 0)
-    def _():
-        other_copy(0, 0, 1).start()
+            forward_near(number)
+
+    @pl.when(band == 2)
+    def _():
+        other_copy(0, 1).start()
 
     @pl.when(band == last)
     def _():
-        other_copy(0, 1, last - 1).start()
-
-    to_across.wait_recv()
-    onward.start()
-    for load in table_loads:
-        load.wait()
-    to_beside.wait_recv()
+        other_copy(1, 2).start()
+
+    @pl.when(either(at_home, at_end))
+    def _():
+        to_across.wait_recv()
+        onward.start()
+
+    @pl.when(jnp.logical_not(early))
+    def _():
+        def one_group(index, carry):
+            forward_near(index)
+            return carry
+
+        lax.fori_loop(0, 2 * halves_count, one_group, 0)
+
     onward.wait_recv()
-
-    def forward(group):
-        forward_group(group, orbital_grid, partner_grid, work, right_forward, left_forward)
-
-    def forward_near(index, carry):
-        forward(
-            (rank + index // halves_count * (beside - rank)) * halves_count + index % halves_count
-        )
-        return carry
-
-    lax.fori_loop(0, 2 * halves_count, forward_near, 0)
+    chosen = shift_index[home]
+    fill_screen([shift_table[axis, chosen] for axis in range(3)], partial)
     for turn_to, half in tail:
 
         @pl.when(jnp.logical_not(early))
@@ -676,18 +707,12 @@
 
         forward(slabs[turn_to] * halves_count + half)
 
-    chosen = shift_index[home]
-    shift = [shift_table[axis, chosen] for axis in range(3)]
-    middle_pairs(shift, work, left_forward, left_inverse)
-
-    @pl.when(band == last)
-    def _():
-        other_copy(1, 1, 0).start()
-
-    @pl.when(band == 1)
-    def _():
-        other_copy(0, 0, 0).wait_recv()
-        other_copy(0, 0, 2, others.at[0]).start()
+    middle_pairs(partial, work, left_forward, left_inverse)
+
+    @pl.when(band == 2)
+    def _():
+        other_copy(1, 2).wait_recv()
+        other_copy(1, 1, others.at[1]).start()
 
     def backward(index, half):
         backward_group(
@@ -703,33 +728,37 @@
             {"fft": beside},
         )
 
-    def far_copy(chunk):
+    def far_copy(cut):
         return remote(
-            outgoing.at[chunk],
-            arriving.at[chunk],
-            far_send.at[chunk],
-            far_recv.at[chunk],
+            outgoing.at[cut_span(cut)],
+            arriving.at[cut_span(cut)],
+            far_send.at[cut],
+            far_recv.at[cut],
             {"fft": across},
         )
 
-    def up_copy(owner, chunk, own=False):
-        held = passed.at[owner, span(chunk)]
+    def up_copy(owner, cut, own=False):
+        held = passed.at[owner, cut_span(cut)]
         return remote(
-            potential.at[span(chunk)] if own else held,
+            potential.at[cut_span(cut)] if own else held,
             held,
-            up_send.at[owner, chunk],
-            up_recv.at[owner, chunk],
+            up_send.at[owner, cut],
+            up_recv.at[owner, cut],
             {"band": band + 1},
         )
 
+    def slice_of(index, cut):
+        return pl.ds(index * planes + cut * slice_size, slice_size)
+
+    per_half = cuts // halves_count
     for half in range(halves_count):
         backward(beside_across, half)
         near_copy(1, beside_across, half).start()
         backward(across, half)
         near_copy(1, beside_across, half).wait_recv()
-        for chunk in of_half(half):
-            outgoing[chunk] = partial[window(across, chunk)] + near[1, span(chunk)]
-            far_copy(chunk).start()
+        for cut in range(half * per_half, (half + 1) * per_half):
+            outgoing[cut_span(cut)] = partial[slice_of(across, cut)] + near[1, cut_span(cut)]
+            far_copy(cut).start()
     for half in range(halves_count):
         backward(beside, half)
         near_copy(0, beside, half).start()
@@ -740,89 +769,82 @@
     for number in range(tallies.shape[0]):
         tallies[number] = zero
 
-    def inner(slot, left, right, chunk):
+    def inner(pairs, right, start, stop):
+        slots = [2 * slot + half for slot, _ in pairs for half in range(2)]
+
         def accumulate(plane, sums):
             straight = right(plane)
-            value = left(plane)
+            sides = (straight, turn(straight))
+            values = [left(plane) for _, left in pairs]
             return tuple(
-                running + jnp.sum((value * other).reshape(rows // 8, 8, lanes), axis=0)
-                for running, other in zip(sums, (straight, turn(straight)))
+                running
+                + jnp.sum((values[n // 2] * sides[n % 2]).reshape(rows // 8, 8, lanes), axis=0)
+                for n, running in enumerate(sums)
             )
 
-        sums = lax.fori_loop(
-            chunk * piece,
-            (chunk + 1) * piece,
-            accumulate,
-            (tallies[2 * slot], tallies[2 * slot + 1]),
-        )
-        tallies[2 * slot] = sums[0]
-        tallies[2 * slot + 1] = sums[1]
+        sums = lax.fori_loop(start, stop, accumulate, tuple(tallies[slot] for slot in slots))
+        for slot, value in zip(slots, sums):
+            tallies[slot] = value
 
     def own_potential(plane):
         return potential[plane]
 
+    def first_potential(plane):
+        return passed[0, plane]
+
     def own_values(plane):
         return orbital_grid[rank * planes + plane]
 
-    holds_first = either(band == 1, band == 2)
-    holds_last = either(band == 0, band == 2)
-
-    def with_others(span_of_chunks, wait):
-        for slot, held in ((0, holds_first), (1, holds_last)):
-
-            @pl.when(held)
-            def _():
-                if wait and slot:
-                    other_copy(0, 1, 0).wait_recv()
-                for chunk in span_of_chunks:
-                    inner(1 + slot, lambda plane: others[slot, plane], own_potential, chunk)
-
-    for chunk in range(chunks):
-        if chunk % per_group == 0:
-            near_copy(0, beside, chunk // per_group).wait_recv()
-        far_copy(chunk).wait_recv()
-        potential[span(chunk)] = (
-            partial[window(rank, chunk)] + near[0, span(chunk)]
-        ) + arriving[chunk]
-
-        @pl.when(band < last - 1 if chunk >= direct else band < last)
+    def other_values(slot):
+        return lambda plane: others[slot, plane]
+
+    for cut in range(cuts):
+        if cut % per_half == 0:
+            near_copy(0, beside, cut // per_half).wait_recv()
+        far_copy(cut).wait_recv()
+        potential[cut_span(cut)] = (
+            partial[slice_of(rank, cut)] + near[0, cut_span(cut)]
+        ) + arriving[cut_span(cut)]
+
+        @pl.when(band < last - 1 if cut >= direct else band < last)
         def _():
-            up_copy(band, chunk, True).start()
-
-        inner(0, own_values, own_potential, chunk)
-        if chunk == chunks - 2:
-
-            @pl.when(band == 2)
-            def _():
-                other_copy(0, 0, 0).wait_recv()
-
-            with_others(range(chunk + 1), True)
-    with_others([chunks - 1], False)
+            up_copy(band, cut, True).start()
+
+        inner([(0, own_values)], own_potential, cut * slice_size, (cut + 1) * slice_size)
+
+    @pl.when(band == 1)
+    def _():
+        other_copy(0, 1).wait_recv()
+        other_copy(1, 1).wait_recv()
+        inner([(1, other_values(0)), (2, other_values(1))], own_potential, 0, planes)
+        for cut in range(cuts):
+            up_copy(0, cut).wait_recv()
+            up_copy(0, cut).start()
+            inner(
+                [(3, own_values), (4, other_values(0)), (5, other_values(1))],
+                first_potential,
+                cut * slice_size,
+                (cut + 1) * slice_size,
+            )
 
     @pl.when(band == 2)
     def _():
-        for chunk in range(chunks):
-            up_copy(1, chunk).wait_recv()
-            if chunk < direct:
-                up_copy(1, chunk).start()
-            inner(3, own_values, lambda plane: passed[1, plane], chunk)
-            inner(4, lambda plane: others[1, plane], lambda plane: passed[1, plane], chunk)
+        inner([(2, other_values(1))], own_potential, 0, planes)
 
     entries = [(i, l) for i in range(bands) for l in range(i + 1)]
-    row_start = band * (band + 1) // 2
     places = (
-        row_start + band,
-        row_start,
+        band * (band + 1) // 2 + band,
+        entries.index((2, 1)),
         entries.index((last, 0)) + band,
-        entries.index((2, 1)),
-        entries.index((last, 1)),
+        entries.index((1, 0)),
+        entries.index((2, 0)),
+        entries.index((last, 0)),
     )
     position = lax.broadcasted_iota(jnp.int32, (8, lanes), 1)
     packed = zero
     for slot, place in enumerate(places):
         for half in range(2):
             value = jnp.sum(tallies[2 * slot + half], axis=1, keepdims=True)
-            value = -value if (slot, half) == (1, 1) else value
             packed = packed + jnp.where(position == 2 * place + half, value, 0.0)
     own_sums[...] = packed
     sum_copies = []
@@ -841,17 +863,12 @@
             sum_copies.append(copy)
     all_sums[band, rank] = packed
 
-    @pl.when(either(band == 1, band == 2))
-    def _():
-        for chunk in range(direct):
-            up_copy(0, chunk).wait_recv()
-            up_copy(0, chunk).start()
-
-    @pl.when(band == 1)
-    def _():
-        for chunk in range(direct, chunks):
-            up_copy(0, chunk).wait_recv()
-            up_copy(0, chunk).start()
+    @pl.when(band == 2)
+    def _():
+        for member in (1, 0):
+            for cut in range(direct):
+                up_copy(member, cut).wait_recv()
+                up_copy(member, cut).start()
 
     for copy in sum_copies:
         copy.wait()
@@ -905,25 +922,29 @@
 
     @pl.when(band == 2)
     def _():
-        for chunk in range(direct, chunks):
-            up_copy(0, chunk).wait_recv()
-            combine(last, 2, (0, 1, None), chunk * piece, (chunk + 1) * piece, put_lifted)
-            up_copy(2, chunk).start()
+        for cut in range(direct, cuts):
+            up_copy(1, cut).wait_recv()
+        for cut in range(direct, cuts):
+            up_copy(0, cut).wait_recv()
+            combine(
+                last, 2, (0, 1, None), cut * slice_size, (cut + 1) * slice_size, put_lifted
+            )
+            up_copy(2, cut).start()
         combine(2, 2, (0, 1, None), 0, planes, put_whole)
 
     @pl.when(band == last)
     def _():
         for member in (2, 1):
-            for chunk in range(direct):
-                up_copy(member, chunk).wait_recv()
-        combine(last, last, (1, 2, None), 0, direct * piece, put_whole)
-        combine(last, last, (None,), direct * piece, planes, put_whole)
-        for chunk in range(direct):
-            up_copy(0, chunk).wait_recv()
-            combine(last, last, (0,), chunk * piece, (chunk + 1) * piece, put_more)
-        for chunk in range(direct, chunks):
-            up_copy(2, chunk).wait_recv()
-            projector[span(chunk)] = projector[span(chunk)] + passed[2, span(chunk)]
+            for cut in range(direct):
+                up_copy(member, cut).wait_recv()
+        combine(last, last, (1, 2, None), 0, direct * slice_size, put_whole)
+        combine(last, last, (None,), direct * slice_size, planes, put_whole)
+        for cut in range(direct):
+            up_copy(0, cut).wait_recv()
+            combine(last, last, (0,), cut * slice_size, (cut + 1) * slice_size, put_more)
+        for cut in range(direct, cuts):
+            up_copy(2, cut).wait_recv()
+            projector[cut_span(cut)] = projector[cut_span(cut)] + passed[2, cut_span(cut)]
 
     for chunk in range(chunks):
 
@@ -946,29 +967,31 @@
                 def _():
                     chain_copy(way, turn_to, chunk).wait_send()
 
-        far_copy(chunk).wait_send()
+    for cut in range(cuts):
+        far_copy(cut).wait_send()
 
         @pl.when(band < last)
         def _():
-            up_copy(band, chunk, True).wait_send()
-
-        if chunk < direct:
+            up_copy(band, cut, True).wait_send()
+
+        if cut < direct:
 
             @pl.when(band == 2)
             def _():
-                up_copy(1, chunk).wait_send()
-
-        @pl.when(band == 1 if chunk >= direct else either(band == 1, band == 2))
+                up_copy(1, cut).wait_send()
+
+        @pl.when(band == 1 if cut >= direct else either(band == 1, band == 2))
         def _():
-            up_copy(0, chunk).wait_send()
-
-    @pl.when(band != 2)
-    def _():
-        other_copy(0, 0, 1).wait_send()
+            up_copy(0, cut).wait_send()
+
+    @pl.when(band == 2)
+    def _():
+        other_copy(0, 1).wait_send()
+        other_copy(1, 1).wait_send()
 
     @pl.when(band == last)
     def _():
-        other_copy(1, 1, 0).wait_send()
+        other_copy(1, 2).wait_send()
 
     for half in range(halves_count):
         near_copy(0, beside, half).wait_send()
@@ -984,7 +1007,7 @@
     halves_count = planes // GROUP
     vmem = pl.BlockSpec(memory_space=pltpu.VMEM)
     smem = pl.BlockSpec(memory_space=pltpu.SMEM)
-    out = jax.ShapeDtypeStruct((planes, rows, lanes), jnp.float32)
+    out = pltpu.VMEM((planes, rows, lanes), jnp.float32)
     grid = pltpu.VMEM((ranks * planes, rows, lanes), jnp.float32)
     slab = pltpu.VMEM((planes, rows, lanes), jnp.float32)
     quarters = pltpu.VMEM((chunks, planes // chunks, rows, lanes), jnp.float32)
@@ -1016,11 +1039,11 @@
             slab,
             quarters,
             slab_list(2),
-            quarters,
-            quarters,
+            slab,
+            slab,
             slab_list(bands - 1),
             slab_list(2),
-            pltpu.VMEM((10, 8, lanes), jnp.float32),
+            pltpu.VMEM((12, 8, lanes), jnp.float32),
             pltpu.VMEM((8, lanes), jnp.float32),
             pltpu.VMEM((bands, ranks, 8, lanes), jnp.float32),
         ]
@@ -1035,14 +1058,14 @@
             dma((ranks, chunks)),
             dma((3,)),
             dma((3,)),
-            dma((2,)),
+            dma((2, bands)),
             dma((2,)),
             dma((2, halves_count)),
             dma((2, halves_count)),
-            dma((chunks,)),
-            dma((chunks,)),
-            dma((bands, chunks)),
-            dma((bands, chunks)),
+            dma((2 * chunks,)),
+            dma((2 * chunks,)),
+            dma((bands, 2 * chunks)),
+            dma((bands, 2 * chunks)),
             dma((bands, ranks)),
             dma((bands, ranks)),
         ],
@@ -1068,7 +1091,7 @@
         count == 1
         and ranks == 4
         and bands == ranks
-        and planes % bands == 0
+        and planes % (2 * bands) == 0
         and planes % GROUP == 0
         and GROUP % (planes // bands) == 0
         and lanes == 2 * rows

time: 88 us -> 79.3 us (0.901)
  Pallas kernels: 84.5 us -> 76.9 us
  local copies, waits for them, and re-layouts: 2.74 us -> 1.59 us
    pallas_call x1, Pallas kernels: 84.5 us -> 76.9 us  [exchange(): pl.pallas_call(functools.partial(exchange_kernel, bands, ranks), name='ex...]
    unnamed x4 -> x2, local copies, waits for them, and re-layouts: 2.74 us -> 1.59 us
where the time goes in v2:
time: 79.3 us; the launch traced here: 79.1 us
  Pallas kernels  76.9 us (97%)
  local copies, waits for them, and re-layouts  1.59 us (2%)
    pallas_call x1, Pallas kernels, exchange(): pl.pallas_call(functools.partial(exchange_kernel, bands, ranks), name='ex...  76.9 us
    unnamed x2, local copies, waits for them, and re-layouts  1.59 us

profile of v2, /device:TPU:24, one launch (start us, length us, event | category | flops | bytes accessed | tf_op | source)
XLA Modules:
  0.0 79.1 jit_solution(5476176423070140666)
XLA Ops:
  0.6 76.9 %exchange.1 = (f32[16,64,128]{2,1,0:T(8,128)S(1)}, f32[16,64,128]{2,1,0:T(8,128)S(1)}) custom-call(f32[3,8]{1,0:T(4,128)} %bitcast.9, s32[4]{0:T(128)} %shift_index.1, f32[16,64,128]{2,1,0:T(8,128)} %bitcast.7, f32[16,64,128]{2,1,0:T(8,128)} %bitcast.8, bf16[256,256]{1,0:T(8,128)(2,1)} %constant.8.clone.right_forward_home, ...), custom_call_target="tpu_custom_call" | custom-call | tf_op jit(solution)/shard_map/exchange/pallas_call | solution.py:1028
  77.5 0.8 %copy.12 = f32[1,16,64,128]{3,2,1,0:T(8,128)} copy(f32[1,16,64,128]{3,2,1,0:T(8,128)S(1)} %bitcast.6) | data formatting | bytes 1048576
  78.3 0.8 %copy.13 = f32[1,16,64,128]{3,2,1,0:T(8,128)} copy(f32[1,16,64,128]{3,2,1,0:T(8,128)S(1)} %bitcast.5) | data formatting | bytes 1048576

commit v3 on v2

--- a/solution.py
+++ b/solution.py
@@ -464,6 +464,8 @@
     cuts = 2 * chunks
     slice_size = planes // cuts
     direct = 4 * cuts // 8
+    lag = cuts // 4
+    held_back = 2 * cuts // 8
     band = lax.axis_index("band")
     rank = lax.axis_index("fft")
     beside = rank + 1 - 2 * (rank % 2)
@@ -653,6 +655,10 @@
             (rank + index // halves_count * (beside - rank)) * halves_count + index % halves_count
         )
 
+    def tabulate():
+        chosen = shift_index[home]
+        fill_screen([shift_table[axis, chosen] for axis in range(3)], partial)
+
     for load in table_loads:
         load.wait()
     to_beside.wait_recv()
@@ -663,7 +669,7 @@
             for chunk in of_half(half):
                 if turn_to == 2:
                     take_detour(at_home, chunk)
-            if number == len(tail) - 1:
+            if number == len(tail) - 2:
 
                 @pl.when(jnp.logical_not(at_home))
                 def _():
@@ -673,6 +679,8 @@
             for chunk in of_half(half):
                 step(turn_to, chunk)
             forward_near(number)
+            if number == 1:
+                tabulate()
 
     @pl.when(band == 2)
     def _():
@@ -694,10 +702,9 @@
             return carry
 
         lax.fori_loop(0, 2 * halves_count, one_group, 0)
+        tabulate()
 
     onward.wait_recv()
-    chosen = shift_index[home]
-    fill_screen([shift_table[axis, chosen] for axis in range(3)], partial)
     for turn_to, half in tail:
 
         @pl.when(jnp.logical_not(early))
@@ -751,19 +758,19 @@
         return pl.ds(index * planes + cut * slice_size, slice_size)
 
     per_half = cuts // halves_count
-    for half in range(halves_count):
+    def halves_of_cuts(half):
+        return range(half * per_half, (half + 1) * per_half)
+
+    def send_half(half):
         backward(beside_across, half)
         near_copy(1, beside_across, half).start()
         backward(across, half)
         near_copy(1, beside_across, half).wait_recv()
-        for cut in range(half * per_half, (half + 1) * per_half):
+        for cut in halves_of_cuts(half):
             outgoing[cut_span(cut)] = partial[slice_of(across, cut)] + near[1, cut_span(cut)]
             far_copy(cut).start()
-    for half in range(halves_count):
         backward(beside, half)
         near_copy(0, beside, half).start()
-    for half in range(halves_count):
-        backward(rank, half)
 
     zero = jnp.zeros((8, lanes), jnp.float32)
     for number in range(tallies.shape[0]):
@@ -782,7 +789,13 @@
                 for n, running in enumerate(sums)
             )
 
-        sums = lax.fori_loop(start, stop, accumulate, tuple(tallies[slot] for slot in slots))
+        sums = lax.fori_loop(
+            start,
+            stop,
+            accumulate,
+            tuple(tallies[slot] for slot in slots),
+            unroll=min(4, stop - start),
+        )
         for slot, value in zip(slots, sums):
             tallies[slot] = value
 
@@ -798,9 +811,7 @@
     def other_values(slot):
         return lambda plane: others[slot, plane]
 
-    for cut in range(cuts):
-        if cut % per_half == 0:
-            near_copy(0, beside, cut // per_half).wait_recv()
+    def finish(cut):
         far_copy(cut).wait_recv()
         potential[cut_span(cut)] = (
             partial[slice_of(rank, cut)] + near[0, cut_span(cut)]
@@ -811,21 +822,54 @@
             up_copy(band, cut, True).start()
 
         inner([(0, own_values)], own_potential, cut * slice_size, (cut + 1) * slice_size)
+        if 0 <= cut - lag < direct:
+
+            @pl.when(band == 2)
+            def _():
+                lift_on(1, cut - lag)
+
+    def lift_on(member, cut):
+        up_copy(member, cut).wait_recv()
+        up_copy(member, cut).start()
+
+    for half in range(halves_count):
+        send_half(half)
+        if half == 0:
+            backward(rank, half)
+            near_copy(0, beside, half).wait_recv()
+            continue
+        for number, cut in enumerate(halves_of_cuts(half - 1)):
+            finish(cut)
+            if number == per_half // 2 - 1:
+                backward(rank, half)
+        near_copy(0, beside, half).wait_recv()
+    for cut in halves_of_cuts(halves_count - 1):
+        finish(cut)
 
     @pl.when(band == 1)
     def _():
+        def pass_on(cut):
+            up_copy(0, cut).wait_recv()
+            if cut < cuts - held_back:
+                up_copy(0, cut).start()
+
+        def with_first(start, stop):
+            inner(
+                [(3, own_values), (4, other_values(0)), (5, other_values(1))],
+                first_potential,
+                start * slice_size,
+                stop * slice_size,
+            )
+
+        for cut in range(per_half):
+            pass_on(cut)
         other_copy(0, 1).wait_recv()
         other_copy(1, 1).wait_recv()
         inner([(1, other_values(0)), (2, other_values(1))], own_potential, 0, planes)
-        for cut in range(cuts):
-            up_copy(0, cut).wait_recv()
-            up_copy(0, cut).start()
-            inner(
-                [(3, own_values), (4, other_values(0)), (5, other_values(1))],
-                first_potential,
-                cut * slice_size,
-                (cut + 1) * slice_size,
-            )
+        with_first(0, per_half)
+        for cut in range(per_half, cuts):
+            pass_on(cut)
+            with_first(cut, cut + 1)
 
     @pl.when(band == 2)
     def _():
@@ -863,12 +907,57 @@
             sum_copies.append(copy)
     all_sums[band, rank] = packed
 
+    @pl.when(band == 1)
+    def _():
+        for cut in range(cuts - held_back, cuts):
+            up_copy(0, cut).start()
+
     @pl.when(band == 2)
     def _():
-        for member in (1, 0):
-            for cut in range(direct):
-                up_copy(member, cut).wait_recv()
-                up_copy(member, cut).start()
+        for cut in range(cuts - lag, direct):
+            lift_on(1, cut)
+        for cut in range(direct):
+            lift_on(0, cut)
+
+    for chunk in range(chunks):
+
+        @pl.when(jnp.logical_not(at_home))
+        def _():
+            gather_copy(chunk).wait_send()
+
+        @pl.when(gives_detour)
+        def _():
+            detour_copy(chunk).wait_send()
+
+        @pl.when(takes_detour)
+        def _():
+            onward_copy(chunk).wait_send()
+
+        for turn_to in range(len(slabs)):
+            for way in (0, 1):
+
+                @pl.when(passes(way, turn_to))
+                def _():
+                    chain_copy(way, turn_to, chunk).wait_send()
+
+    @pl.when(band == 2)
+    def _():
+        other_copy(0, 1).wait_send()
+        other_copy(1, 1).wait_send()
+
+    @pl.when(band == last)
+    def _():
+        other_copy(1, 2).wait_send()
+
+    for half in range(halves_count):
+        near_copy(0, beside, half).wait_send()
+        near_copy(1, beside_across, half).wait_send()
+    to_across.wait_send()
+    to_beside.wait_send()
+    onward.wait_send()
+
+    for cut in range(cuts):
+        far_copy(cut).wait_send()
 
     for copy in sum_copies:
         copy.wait()
@@ -903,7 +992,7 @@
             put(plane, sum_straight + turn(sum_turned))
             return carry
 
-        lax.fori_loop(start, stop, one_plane, 0)
+        lax.fori_loop(start, stop, one_plane, 0, unroll=min(4, stop - start))
 
     def put_whole(plane, value):
         projector[plane] = value
@@ -946,30 +1035,7 @@
             up_copy(2, cut).wait_recv()
             projector[cut_span(cut)] = projector[cut_span(cut)] + passed[2, cut_span(cut)]
 
-    for chunk in range(chunks):
-
-        @pl.when(jnp.logical_not(at_home))
-        def _():
-            gather_copy(chunk).wait_send()
-
-        @pl.when(gives_detour)
-        def _():
-            detour_copy(chunk).wait_send()
-
-        @pl.when(takes_detour)
-        def _():
-            onward_copy(chunk).wait_send()
-
-        for turn_to in range(len(slabs)):
-            for way in (0, 1):
-
-                @pl.when(passes(way, turn_to))
-                def _():
-                    chain_copy(way, turn_to, chunk).wait_send()
-
     for cut in range(cuts):
-        far_copy(cut).wait_send()
-
         @pl.when(band < last)
         def _():
             up_copy(band, cut, True).wait_send()
@@ -983,22 +1049,6 @@
         @pl.when(band == 1 if cut >= direct else either(band == 1, band == 2))
         def _():
             up_copy(0, cut).wait_send()
-
-    @pl.when(band == 2)
-    def _():
-        other_copy(0, 1).wait_send()
-        other_copy(1, 1).wait_send()
-
-    @pl.when(band == last)
-    def _():
-        other_copy(1, 2).wait_send()
-
-    for half in range(halves_count):
-        near_copy(0, beside, half).wait_send()
-        near_copy(1, beside_across, half).wait_send()
-    to_across.wait_send()
-    to_beside.wait_send()
-    onward.wait_send()
 
 
 def exchange(bands, ranks, orbital, partner, shift_table, shift_index):

time: 79.3 us -> 76.4 us (0.963)
  Pallas kernels: 76.9 us -> 74 us
    pallas_call x1, Pallas kernels: 76.9 us -> 74 us  [exchange(): pl.pallas_call(functools.partial(exchange_kernel, bands, ranks), name='ex...]
where the time goes in v3:
time: 76.4 us; the launch traced here: 76.2 us
  Pallas kernels  74 us (97%)
  local copies, waits for them, and re-layouts  1.59 us (2%)
    pallas_call x1, Pallas kernels, exchange(): pl.pallas_call(functools.partial(exchange_kernel, bands, ranks), name='ex...  74 us
    unnamed x2, local copies, waits for them, and re-layouts  1.59 us

profile of v3, /device:TPU:24, one launch (start us, length us, event | category | flops | bytes accessed | tf_op | source)
XLA Modules:
  0.0 76.2 jit_solution(5460352968251599144)
XLA Ops:
  0.6 74.0 %exchange.1 = (f32[16,64,128]{2,1,0:T(8,128)S(1)}, f32[16,64,128]{2,1,0:T(8,128)S(1)}) custom-call(f32[3,8]{1,0:T(4,128)} %bitcast.9, s32[4]{0:T(128)} %shift_index.1, f32[16,64,128]{2,1,0:T(8,128)} %bitcast.7, f32[16,64,128]{2,1,0:T(8,128)} %bitcast.8, bf16[256,256]{1,0:T(8,128)(2,1)} %constant.8.clone.right_forward_home, ...), custom_call_target="tpu_custom_call" | custom-call | tf_op jit(solution)/shard_map/exchange/pallas_call | solution.py:1078
  74.6 0.8 %copy.12 = f32[1,16,64,128]{3,2,1,0:T(8,128)} copy(f32[1,16,64,128]{3,2,1,0:T(8,128)S(1)} %bitcast.6) | data formatting | bytes 1048576
  75.4 0.8 %copy.13 = f32[1,16,64,128]{3,2,1,0:T(8,128)} copy(f32[1,16,64,128]{3,2,1,0:T(8,128)S(1)} %bitcast.5) | data formatting | bytes 1048576

commit v4 on v3

--- a/solution.py
+++ b/solution.py
@@ -428,6 +428,7 @@
     arriving,
     passed,
     others,
+    tops,
     tallies,
     own_sums,
     all_sums,
@@ -446,6 +447,10 @@
     grid_recv,
     other_send,
     other_recv,
+    third_send,
+    third_recv,
+    top_send,
+    top_recv,
     near_send,
     near_recv,
     far_send,
@@ -466,6 +471,8 @@
     direct = 4 * cuts // 8
     lag = cuts // 4
     held_back = 2 * cuts // 8
+    top = 4 * cuts // 8
+    split = (cuts - top) * slice_size
     band = lax.axis_index("band")
     rank = lax.axis_index("fft")
     beside = rank + 1 - 2 * (rank % 2)
@@ -647,6 +654,28 @@
             {"band": where},
         )
 
+    def third_copy(number):
+        place = pl.ds(split, planes - split) if number == 0 else pl.ds(0, split)
+        held = others.at[1, place]
+        return remote(
+            held, held, third_send.at[number], third_recv.at[number], {"band": 1}
+        )
+
+    def top_copy(member):
+        rest = pl.ds(split, planes - split)
+        source = (
+            orbital_grid.at[pl.ds(rank * planes + split, planes - split)]
+            if member == 0
+            else others.at[member - 1, rest]
+        )
+        return remote(
+            source,
+            tops.at[member],
+            top_send.at[member],
+            top_recv.at[member],
+            {"band": 0},
+        )
+
     def forward(group):
         forward_group(group, orbital_grid, partner_grid, work, right_forward, left_forward)
 
@@ -719,7 +748,8 @@
     @pl.when(band == 2)
     def _():
         other_copy(1, 2).wait_recv()
-        other_copy(1, 1, others.at[1]).start()
+        for number in range(2):
+            third_copy(number).start()
 
     def backward(index, half):
         backward_group(
@@ -817,7 +847,9 @@
             partial[slice_of(rank, cut)] + near[0, cut_span(cut)]
         ) + arriving[cut_span(cut)]
 
-        @pl.when(band < last - 1 if cut >= direct else band < last)
+        sends = band < last - 1 if cut >= direct else band < last
+
+        @pl.when(both(sends, band > 0) if cut >= cuts - held_back else sends)
         def _():
             up_copy(band, cut, True).start()
 
@@ -828,6 +860,13 @@
             def _():
                 lift_on(1, cut - lag)
 
+        if cut == cuts // 2:
+
+            @pl.when(band == 1)
+            def _():
+                other_copy(0, 1).wait_recv()
+                top_copy(1).start()
+
     def lift_on(member, cut):
         up_copy(member, cut).wait_recv()
         up_copy(member, cut).start()
@@ -835,6 +874,11 @@
     for half in range(halves_count):
         send_half(half)
         if half == 0:
+
+            @pl.when(band == 1)
+            def _():
+                top_copy(0).start()
+
             backward(rank, half)
             near_copy(0, beside, half).wait_recv()
             continue
@@ -850,8 +894,7 @@
     def _():
         def pass_on(cut):
             up_copy(0, cut).wait_recv()
-            if cut < cuts - held_back:
-                up_copy(0, cut).start()
+            up_copy(0, cut).start()
 
         def with_first(start, stop):
             inner(
@@ -861,19 +904,34 @@
                 stop * slice_size,
             )
 
+        third_copy(0).wait_recv()
+        top_copy(2).start()
         for cut in range(per_half):
             pass_on(cut)
-        other_copy(0, 1).wait_recv()
-        other_copy(1, 1).wait_recv()
+        third_copy(1).wait_recv()
         inner([(1, other_values(0)), (2, other_values(1))], own_potential, 0, planes)
         with_first(0, per_half)
-        for cut in range(per_half, cuts):
+        for cut in range(per_half, cuts - top):
             pass_on(cut)
             with_first(cut, cut + 1)
 
     @pl.when(band == 2)
     def _():
         inner([(2, other_values(1))], own_potential, 0, planes)
+
+    @pl.when(band == 0)
+    def _():
+        for member in range(3):
+            top_copy(member).wait_recv()
+        inner(
+            [
+                (3 + member, lambda plane, member=member: tops[member, plane - split])
+                for member in range(3)
+            ],
+            own_potential,
+            split,
+            planes,
+        )
 
     entries = [(i, l) for i in range(bands) for l in range(i + 1)]
     places = (
@@ -907,9 +965,15 @@
             sum_copies.append(copy)
     all_sums[band, rank] = packed
 
+    @pl.when(band == 0)
+    def _():
+        for cut in range(cuts - held_back, cuts):
+            up_copy(0, cut, True).start()
+
     @pl.when(band == 1)
     def _():
-        for cut in range(cuts - held_back, cuts):
+        for cut in range(cuts - top, cuts):
+            up_copy(0, cut).wait_recv()
             up_copy(0, cut).start()
 
     @pl.when(band == 2)
@@ -943,7 +1007,13 @@
     @pl.when(band == 2)
     def _():
         other_copy(0, 1).wait_send()
-        other_copy(1, 1).wait_send()
+        for number in range(2):
+            third_copy(number).wait_send()
+
+    @pl.when(band == 1)
+    def _():
+        for member in range(3):
+            top_copy(member).wait_send()
 
     @pl.when(band == last)
     def _():
@@ -1093,6 +1163,7 @@
             slab,
             slab_list(bands - 1),
             slab_list(2),
+            pltpu.VMEM((3, 4 * (planes // (2 * chunks)), rows, lanes), jnp.float32),
             pltpu.VMEM((12, 8, lanes), jnp.float32),
             pltpu.VMEM((8, lanes), jnp.float32),
             pltpu.VMEM((bands, ranks, 8, lanes), jnp.float32),
@@ -1110,6 +1181,10 @@
             dma((3,)),
             dma((2, bands)),
             dma((2,)),
+            dma((2,)),
+            dma((2,)),
+            dma((3,)),
+            dma((3,)),
             dma((2, halves_count)),
             dma((2, halves_count)),
             dma((2 * chunks,)),

time: 76.4 us -> 74.5 us (0.975)
  Pallas kernels: 74 us -> 72.1 us
    pallas_call x1, Pallas kernels: 74 us -> 72.1 us  [exchange(): pl.pallas_call(functools.partial(exchange_kernel, bands, ranks), name='ex...]
where the time goes in v4:
time: 74.5 us; the launch traced here: 74.3 us
  Pallas kernels  72.1 us (97%)
  local copies, waits for them, and re-layouts  1.59 us (2%)
    pallas_call x1, Pallas kernels, exchange(): pl.pallas_call(functools.partial(exchange_kernel, bands, ranks), name='ex...  72.1 us
    unnamed x2, local copies, waits for them, and re-layouts  1.59 us

profile of v4, /device:TPU:24, one launch (start us, length us, event | category | flops | bytes accessed | tf_op | source)
XLA Modules:
  0.0 74.3 jit_solution(16732050508399762912)
XLA Ops:
  0.6 72.1 %exchange.1 = (f32[16,64,128]{2,1,0:T(8,128)S(1)}, f32[16,64,128]{2,1,0:T(8,128)S(1)}) custom-call(f32[3,8]{1,0:T(4,128)} %bitcast.9, s32[4]{0:T(128)} %shift_index.1, f32[16,64,128]{2,1,0:T(8,128)} %bitcast.7, f32[16,64,128]{2,1,0:T(8,128)} %bitcast.8, bf16[256,256]{1,0:T(8,128)(2,1)} %constant.8.clone.right_forward_home, ...), custom_call_target="tpu_custom_call" | custom-call | tf_op jit(solution)/shard_map/exchange/pallas_call | solution.py:1148
  72.8 0.8 %copy.12 = f32[1,16,64,128]{3,2,1,0:T(8,128)} copy(f32[1,16,64,128]{3,2,1,0:T(8,128)S(1)} %bitcast.6) | data formatting | bytes 1048576
  73.6 0.8 %copy.13 = f32[1,16,64,128]{3,2,1,0:T(8,128)} copy(f32[1,16,64,128]{3,2,1,0:T(8,128)S(1)} %bitcast.5) | data formatting | bytes 1048576

commit v5 on v4

--- a/solution.py
+++ b/solution.py
@@ -401,7 +401,7 @@
         work[2 * pair + 1] = fields[1]
         return carry
 
-    lax.fori_loop(0, columns // 2, one_pair, 0, unroll=16)
+    lax.fori_loop(0, columns // 2, one_pair, 0, unroll=32)
 
 
 def exchange_kernel(
@@ -1200,9 +1200,34 @@
     )(shift_table.T, shift_index, orbital, partner, *tables)
 
 
+def settle_kernel(potential, projector, potential_home, projector_home, sem):
+    copies = [
+        pltpu.make_async_copy(here, home, sem.at[number])
+        for number, (here, home) in enumerate(
+            ((potential, potential_home), (projector, projector_home))
+        )
+    ]
+    for copy in copies:
+        copy.start()
+    for copy in copies:
+        copy.wait()
+
+
+def settle(potential, projector):
+    out = jax.ShapeDtypeStruct(potential.shape, jnp.float32)
+    return pl.pallas_call(
+        settle_kernel,
+        name="settle",
+        out_shape=(out, out),
+        in_specs=[pl.BlockSpec(memory_space=pltpu.VMEM)] * 2,
+        out_specs=(pl.BlockSpec(memory_space=pl.ANY),) * 2,
+        scratch_shapes=[pltpu.SemaphoreType.DMA((2,))],
+    )(*[pltpu.with_memory_space_constraint(value, pltpu.VMEM) for value in (potential, projector)])
+
+
 def paired_body(bands, ranks, orbitals, partners, shift_table, shift_index):
-    potential, projector = exchange(
-        bands, ranks, orbitals[0], partners[0], shift_table, shift_index
+    potential, projector = settle(
+        *exchange(bands, ranks, orbitals[0], partners[0], shift_table, shift_index)
     )
     return (potential[None], projector[None])
 

time: 74.5 us -> 73.5 us (0.987)
  local copies, waits for them, and re-layouts: 1.59 us -> 0 us
    unnamed x2 -> x0, local copies, waits for them, and re-layouts: 1.59 us -> none
    pallas_call x0 -> x1, Pallas kernels: none -> 0.99 us  [settle(): pl.pallas_call(settle_kernel, name='settle', out_shape=(out, out), in_spe...]
where the time goes in v5:
time: 73.5 us; the launch traced here: 73.3 us
  Pallas kernels  72.7 us (99%)
    pallas_call x1, Pallas kernels, exchange(): pl.pallas_call(functools.partial(exchange_kernel, bands, ranks), name='ex...  71.7 us

profile of v5, /device:TPU:24, one launch (start us, length us, event | category | flops | bytes accessed | tf_op | source)
XLA Modules:
  0.0 73.3 jit_solution(16382459209288234809)
XLA Ops:
  0.6 71.7 %exchange.1 = (f32[16,64,128]{2,1,0:T(8,128)S(1)}, f32[16,64,128]{2,1,0:T(8,128)S(1)}) custom-call(f32[3,8]{1,0:T(4,128)} %bitcast.7, s32[4]{0:T(128)} %shift_index.1, f32[16,64,128]{2,1,0:T(8,128)} %bitcast.5, f32[16,64,128]{2,1,0:T(8,128)} %bitcast.6, bf16[256,256]{1,0:T(8,128)(2,1)} %constant.8.clone.right_forward_home, ...), custom_call_target="tpu_custom_call" | custom-call | tf_op jit(solution)/shard_map/exchange/pallas_call | solution.py:1148
  72.3 1.0 %settle.1 = (f32[16,64,128]{2,1,0:T(8,128)}, f32[16,64,128]{2,1,0:T(8,128)}) custom-call(f32[16,64,128]{2,1,0:T(8,128)S(1)} %get-tuple-element.6.potential, f32[16,64,128]{2,1,0:T(8,128)S(1)} %get-tuple-element.7.projector), custom_call_target="tpu_custom_call" | custom-call | tf_op jit(solution)/shard_map/settle/pallas_call | solution.py:1218

commit v6 on v5

--- a/solution.py
+++ b/solution.py
@@ -607,21 +607,6 @@
     def of_half(half):
         return range(half * per_group, (half + 1) * per_group)
 
-    partner_load.wait()
-    for chunk in range(chunks):
-
-        @pl.when(jnp.logical_not(at_home))
-        def _():
-            gather_copy(chunk).start()
-
-        @pl.when(gives_detour)
-        def _():
-            detour_copy(chunk).start()
-
-    @pl.when(at_home)
-    def _():
-        home_load.wait()
-
     own_slab.wait()
     own_orbital = orbital_grid.at[slab(rank)]
     to_across = remote(own_orbital, own_orbital, grid_send.at[0], grid_recv.at[0], {"fft": across})
@@ -630,7 +615,23 @@
     onward = remote(
         other_orbital, other_orbital, grid_send.at[2], grid_recv.at[2], {"fft": beside}
     )
-    to_across.start()
+    pl.when(jnp.logical_not(at_end))(to_across.start)
+    partner_load.wait()
+    for chunk in range(chunks):
+
+        @pl.when(jnp.logical_not(at_home))
+        def _():
+            gather_copy(chunk).start()
+
+        @pl.when(gives_detour)
+        def _():
+            detour_copy(chunk).start()
+
+    @pl.when(at_home)
+    def _():
+        home_load.wait()
+
+    pl.when(at_end)(to_across.start)
     to_beside.start()
 
     def take_detour(condition, chunk):
@@ -698,7 +699,7 @@
             for chunk in of_half(half):
                 if turn_to == 2:
                     take_detour(at_home, chunk)
-            if number == len(tail) - 2:
+            if number == 0:
 
                 @pl.when(jnp.logical_not(at_home))
                 def _():

time: 73.5 us -> 75.9 us (1.033)
  Pallas kernels: 72.7 us -> 75.1 us
    pallas_call x1, Pallas kernels: 71.7 us -> 74.1 us  [exchange(): pl.pallas_call(functools.partial(exchange_kernel, bands, ranks), name='ex...]
where the time goes in v6:
time: 75.9 us; the launch traced here: 75.7 us
  Pallas kernels  75.1 us (99%)
    pallas_call x1, Pallas kernels, exchange(): pl.pallas_call(functools.partial(exchange_kernel, bands, ranks), name='ex...  74.1 us

profile of v6, /device:TPU:24, one launch (start us, length us, event | category | flops | bytes accessed | tf_op | source)
XLA Modules:
  0.0 75.7 jit_solution(13836854993717303860)
XLA Ops:
  0.6 74.1 %exchange.1 = (f32[16,64,128]{2,1,0:T(8,128)S(1)}, f32[16,64,128]{2,1,0:T(8,128)S(1)}) custom-call(f32[3,8]{1,0:T(4,128)} %bitcast.7, s32[4]{0:T(128)} %shift_index.1, f32[16,64,128]{2,1,0:T(8,128)} %bitcast.5, f32[16,64,128]{2,1,0:T(8,128)} %bitcast.6, bf16[256,256]{1,0:T(8,128)(2,1)} %constant.8.clone.right_forward_home, ...), custom_call_target="tpu_custom_call" | custom-call | tf_op jit(solution)/shard_map/exchange/pallas_call | solution.py:1149
  74.7 1.0 %settle.1 = (f32[16,64,128]{2,1,0:T(8,128)}, f32[16,64,128]{2,1,0:T(8,128)}) custom-call(f32[16,64,128]{2,1,0:T(8,128)S(1)} %get-tuple-element.6.potential, f32[16,64,128]{2,1,0:T(8,128)S(1)} %get-tuple-element.7.projector), custom_call_target="tpu_custom_call" | custom-call | tf_op jit(solution)/shard_map/settle/pallas_call | solution.py:1219
